TPU v7x, 16 devices: a whole 2x2x2 slice. The times are simulated.
16 devices in a mesh: rep: 1, dp: 16 (over x, y, z, core).
Axes of the slice: x: 2, y: 2, z: 2, core: 2. Of those that a mesh axis runs over, the one named last changes fastest.
Arguments:
- x: bfloat16 [16, 2048, 1024], P(('rep', 'dp'))
- dy: bfloat16 [16, 2048, 1024], P(('rep', 'dp'))
- w_gate: bfloat16 [2, 1024, 3200], replicated
- w_up: bfloat16 [2, 1024, 3200], replicated
- w_down: bfloat16 [2, 3200, 1024], replicated
- m_w_gate: float32 [2, 1024, 3200], replicated
- m_w_up: float32 [2, 1024, 3200], replicated
- m_w_down: float32 [2, 3200, 1024], replicated
- v_w_gate: float32 [2, 1024, 3200], replicated
- v_w_up: float32 [2, 1024, 3200], replicated
- v_w_down: float32 [2, 3200, 1024], replicated
Outputs:
- output 1: bfloat16 [2, 1024, 3200], P('rep')
- output 2: bfloat16 [2, 1024, 3200], P('rep')
- output 3: bfloat16 [2, 3200, 1024], P('rep')
- output 4: float32 [2, 1024, 3200], P('rep')
- output 5: float32 [2, 1024, 3200], P('rep')
- output 6: float32 [2, 3200, 1024], P('rep')
- output 7: float32 [2, 1024, 3200], P('rep')
- output 8: float32 [2, 1024, 3200], P('rep')
- output 9: float32 [2, 3200, 1024], P('rep')
All inputs are finite; a program needn't handle non-finite values.
Results may differ from a plain program's by a relative error of at most 0.022.
Values are sent between devices in bfloat16 or wider.
A program may use at most 2.75 GiB of HBM per device.

v0:
```python
import jax
import jax.numpy as jnp
from jax import lax
from jax.sharding import PartitionSpec as P

NAMES = ("w_gate", "w_up", "w_down")


def matmul(a, w):
    return jnp.dot(a, w, preferred_element_type=jnp.float32).astype(jnp.bfloat16)


def normed(h):
    wide = h.astype(jnp.float32)
    scale = lax.rsqrt(jnp.mean(wide**2, -1, keepdims=True) + 1e-6)
    return (wide * scale).astype(jnp.bfloat16)


def layer(h, w):
    a = normed(h)
    gate = jnp.dot(a, w["w_gate"], preferred_element_type=jnp.float32)
    up = jnp.dot(a, w["w_up"], preferred_element_type=jnp.float32)
    return h + matmul((jax.nn.silu(gate) * up).astype(jnp.bfloat16), w["w_down"])


def adamw(w, m, v, g):
    m = 0.9 * m + 0.1 * g
    v = 0.95 * v + 0.05 * g * g
    step = m * lax.rsqrt(v + 1e-8) + 0.1 * w
    return (w - 0.02 * step).astype(jnp.bfloat16), m, v


def solution(mesh):
    def step(x, dy, *arrays):
        weights, m, v = (arrays[i : i + 3] for i in (0, 3, 6))
        layers = weights[0].shape[0]
        h, kept = x[0], []
        for number in range(layers):
            kept.append(h)
            h = layer(h, {name: w[number] for name, w in zip(NAMES, weights, strict=True)})
        by_h, summed = dy[0], [None] * layers
        for number in reversed(range(layers)):
            _, back = jax.vjp(lambda w, h: layer(h, w), {name: w[number] for name, w in zip(NAMES, weights, strict=True)}, kept[number])
            by_w, by_h = back(by_h)
            summed[number] = [lax.psum(by_w[name], "dp") for name in NAMES]
        gradients = [jnp.stack([summed[number][i] for number in range(layers)]).astype(jnp.float32) for i in range(3)]
        new = [adamw(w.astype(jnp.float32), m, v, g) for w, m, v, g in zip(weights, m, v, gradients, strict=True)]
        return tuple(one[which] for which in range(3) for one in new)

    return jax.shard_map(
        step,
        mesh=mesh,
        in_specs=(P(("rep", "dp"), None, None),) * 2 + (P(None, None, None),) * 9,
        out_specs=(P("rep", None, None),) * 9,
        check_vma=False,
    )
```

profile of v0, /device:TPU:0, one launch (start us, length us, event | category | flops | bytes accessed | tf_op | source)
XLA Modules:
  0.0 913.9 jit_solution(9041817674536290881)
XLA Ops:
  7.2 0.0 all-reduce.3.cloned.1.call-start
  7.2 6.5 copy.20
  13.7 3.1 fusion.30
  16.8 6.5 copy.21
  23.3 20.9 %convolution_convert_fusion.1 = bf16[2048,3200]{1,0:T(8,128)(2,1)} fusion(bf16[2,3200,1024]{2,1,0:T(8,128)(2,1)} %param.15, bf16[1,2048,1024]{2,1,0:T(8,128)(2,1)} %param.12), kind=kOutput, calls=%fused_computation.50 | convolution fusion | flops 13428326400 | bytes 23855104 | tf_op jit(solution)/shard_map/transpose(jvp())/dot_general | solution.py:10
  44.2 20.9 %fusion.56 = f32[2048,3200]{1,0:T(8,128)} fusion(bf16[2,1024,3200]{2,1,0:T(8,128)(2,1)} %param.13, bf16[1,2048,1024]{2,1,0:T(8,128)(2,1)S(1)} %copy-done.3, f32[2048]{0:T(1024)S(1)} %add_rsqrt_fusion), kind=kOutput, calls=%fused_computation.90 | convolution fusion | flops 13428064256 | bytes 36970496 | tf_op jit(solution)/shard_map/dot_general | solution.py:21
  65.1 32.2 %multiply_convert_fusion.1 = (bf16[2048,3200]{1,0:T(8,128)(2,1)}, f32[2048,3200]{1,0:T(8,128)}) fusion(f32[2048,3200]{1,0:T(8,128)} %fusion.56, bf16[2,1024,3200]{2,1,0:T(8,128)(2,1)} %param.14, bf16[1,2048,1024]{2,1,0:T(8,128)(2,1)} %param.11, f32[2048]{0:T(1024)S(1)} %add_rsqrt_fusion), kind=kOutput, calls=%fused_computation.44 | convolution fusion | flops 13467385856 | bytes 76292096 | tf_op jit(solution)/shard_map/dot_general | solution.py:22
  97.4 21.9 %fusion.34 = (f32[2048]{0:T(1024)S(1)}, bf16[2048,1024]{0,1:T(8,128)(2,1)}) fusion(bf16[2048,3200]{1,0:T(8,128)(2,1)} %get-tuple-element.24, bf16[2,3200,1024]{2,1,0:T(8,128)(2,1)} %param.15, bf16[1,2048,1024]{1,2,0:T(8,128)(2,1)} %copy.20), kind=kOutput, calls=%fused_computation.67 | convolution fusion | flops 13432256512 | bytes 28057600 | tf_op jit(solution)/shard_map/dot_general | solution.py:10
  119.2 23.3 %fusion.43 = f32[2048,3200]{1,0:T(8,128)} fusion(bf16[2,1024,3200]{2,1,0:T(8,128)(2,1)} %param.14, bf16[2048,1024]{0,1:T(8,128)(2,1)} %get-tuple-element.27, f32[2048]{0:T(1024)S(1)} %fusion.92), kind=kOutput, calls=%fused_computation.77 | convolution fusion | flops 13428064256 | bytes 36970496 | tf_op jit(solution)/shard_map/jvp()/dot_general | solution.py:22
  142.6 39.0 %fusion.14 = (bf16[2048,3200]{1,0:T(8,128)(2,1)}, f32[2048,3200]{1,0:T(8,128)}) fusion(f32[2048,3200]{1,0:T(8,128)} %fusion.43, bf16[2048,3200]{1,0:T(8,128)(2,1)} %convolution_convert_fusion.1, bf16[2,1024,3200]{2,1,0:T(8,128)(2,1)} %param.13, bf16[2048,1024]{0,1:T(8,128)(2,1)} %get-tuple-element.27, f32[2048]{0:T(1024)S(1)} %fusion.92), kind=kOutput, calls=%fused_computation.32 | convolution fusion | flops 13506707456 | bytes 89399296 | tf_op jit(solution)/shard_map/jvp()/dot_general | solution.py:21
  181.5 22.6 %fusion.27 = bf16[2048,1024]{0,1:T(8,128)(2,1)} fusion(bf16[2048,3200]{1,0:T(8,128)(2,1)} %convolution_convert_fusion.1, bf16[2,1024,3200]{2,1,0:T(8,128)(2,1)} %param.14, f32[2048,3200]{1,0:T(8,128)} %get-tuple-element.29), kind=kOutput, calls=%fused_computation.48 | convolution fusion | flops 13461094400 | bytes 50069504 | tf_op jit(solution)/shard_map/transpose(jvp())/dot_general | solution.py:22
  204.2 24.2 %fusion.64 = bf16[1,1024,3200]{2,1,0:T(8,128)(2,1)} fusion(bf16[2048,3200]{1,0:T(8,128)(2,1)} %convolution_convert_fusion.1, bf16[2048,1024]{0,1:T(8,128)(2,1)S(1)} %copy-done.2, f32[2048]{0:T(1024)S(1)} %fusion.92, f32[2048,3200]{1,0:T(8,128)} %get-tuple-element.29), kind=kOutput, calls=%fused_computation.98 | convolution fusion | flops 13470662656 | bytes 50077696 | tf_op jit(solution)/shard_map/transpose(jvp())/dot_general | solution.py:22
  228.4 25.7 %fusion.65 = bf16[1,3200,1024]{2,1,0:T(8,128)(2,1)} fusion(f32[2048,3200]{1,0:T(8,128)} %fusion.43, bf16[1,2048,1024]{2,1,0:T(8,128)(2,1)} %param.12, f32[2048,3200]{1,0:T(8,128)} %get-tuple-element.29), kind=kOutput, calls=%fused_computation.99 | convolution fusion | flops 13464371200 | bytes 63176704 | tf_op jit(solution)/shard_map/transpose(jvp())/dot_general | solution.py:10
  254.0 21.2 %fusion.61 = bf16[1,1024,3200]{2,1,0:T(8,128)(2,1)} fusion(bf16[2048,3200]{1,0:T(8,128)(2,1)} %get-tuple-element.28, bf16[2048,1024]{0,1:T(8,128)(2,1)} %get-tuple-element.27, f32[2048]{0:T(1024)S(1)} %fusion.92), kind=kOutput, calls=%fused_computation.95 | convolution fusion | flops 13428064256 | bytes 23863296 | tf_op jit(solution)/shard_map/transpose(jvp())/dot_general | solution.py:21
  275.3 22.8 %fusion.36 = (f32[2048]{0:T(1024)S(1)}, bf16[2048,1024]{0,1:T(8,128)(2,1)}) fusion(bf16[2048,1024]{0,1:T(8,128)(2,1)} %get-tuple-element.27, bf16[2048,1024]{0,1:T(8,128)(2,1)} %fusion.27, bf16[2048,3200]{1,0:T(8,128)(2,1)} %get-tuple-element.28, bf16[2,1024,3200]{2,1,0:T(8,128)(2,1)} %param.13), kind=kOutput, calls=%fused_computation.69 | convolution fusion | flops 13432256512 | bytes 32251904 | tf_op jit(solution)/shard_map/transpose(jvp())/dot_general | solution.py:21
  298.1 6.6 fusion.77
  304.7 21.1 %convolution_convert_fusion = bf16[2048,3200]{1,0:T(8,128)(2,1)} fusion(bf16[2048,1024]{0,1:T(8,128)(2,1)} %fusion.77, bf16[2,3200,1024]{2,1,0:T(8,128)(2,1)} %param.15), kind=kOutput, calls=%fused_computation.49 | convolution fusion | flops 13428326400 | bytes 23855104 | tf_op jit(solution)/shard_map/transpose(jvp())/dot_general | solution.py:10
  325.8 21.2 %fusion.62 = bf16[1,3200,1024]{2,1,0:T(8,128)(2,1)} fusion(bf16[2048,3200]{1,0:T(8,128)(2,1)} %get-tuple-element.24, bf16[2048,1024]{0,1:T(8,128)(2,1)} %fusion.77), kind=kOutput, calls=%fused_computation.96 | convolution fusion | flops 13425049600 | bytes 23855104 | tf_op jit(solution)/shard_map/transpose(jvp())/dot_general | solution.py:10
  347.0 24.2 %fusion.63 = bf16[1,1024,3200]{2,1,0:T(8,128)(2,1)} fusion(bf16[2048,3200]{1,0:T(8,128)(2,1)} %convolution_convert_fusion, f32[2048,3200]{1,0:T(8,128)} %fusion.56, bf16[1,2048,1024]{1,2,0:T(8,128)(2,1)S(1)} %copy-done.1, f32[2048]{0:T(1024)S(1)} %copy-done.7), kind=kOutput, calls=%fused_computation.97 | convolution fusion | flops 13470662656 | bytes 50077696 | tf_op jit(solution)/shard_map/transpose(jvp())/dot_general | solution.py:22
  371.2 29.7 %fusion.66 = bf16[1,1024,3200]{2,1,0:T(8,128)(2,1)} fusion(f32[2048,3200]{1,0:T(8,128)} %fusion.56, f32[2048,3200]{1,0:T(8,128)} %get-tuple-element.25, bf16[2048,3200]{1,0:T(8,128)(2,1)} %convolution_convert_fusion, bf16[1,2048,1024]{1,2,0:T(8,128)(2,1)S(1)} %copy-done.1, f32[2048]{0:T(1024)S(1)} %copy-done.7), kind=kOutput, calls=%fused_computation.100 | convolution fusion | flops 13503430656 | bytes 76292096 | tf_op jit(solution)/shard_map/transpose(jvp())/dot_general | solution.py:21
  400.9 0.0 all-reduce.3.cloned.1.call-update
  400.9 364.6 %all-reduce.3.cloned.1.call-done = (bf16[1,1024,3200]{2,1,0:T(8,128)(2,1)}, bf16[1,1024,3200]{2,1,0:T(8,128)(2,1)}, bf16[1,1024,3200]{2,1,0:T(8,128)(2,1)}, bf16...) async-done(((bf16[1,1024,3200]{2,1,0:T(8,128)(2,1)}, bf16[1,1024,3200]{2,1,0:T(8,128)(2,1)}, ...) | async-done | bytes 39321616 | tf_op jit(solution)/shard_map/psum | solution.py:45
  765.5 49.7 %fusion.11 = (bf16[2,3200,1024]{2,1,0:T(8,128)(2,1)}, f32[2,3200,1024]{2,1,0:T(8,128)}, f32[2,3200,1024]{2,1,0:T(8,128)}) fusion(bf16[2,3200,1024]{2,1,0:T(8,128)(2,1)} %param.15, bf16[1,3200,1024]{2,1,0:T(8,128)(2,1)} %get-tuple-element.13, bf16[1,3200,1024]{2,1,0:T(8,128)(2,1)} %get-tuple-element.14, f32[2,3200,1024]{2,1,0:T(8,128)} %param.21, ...), kind=kLoop, calls=%fused_computation.29 | loop fusion | flops 124518400 | bytes 144179200 | tf_op jit(solution)/shard_map/convert_element_type | solution.py:30
  815.2 91.6 %fusion.2 = (bf16[2,1024,3200]{2,1,0:T(8,128)(2,1)}, f32[2,1024,3200]{2,1,0:T(8,128)}, f32[2,1024,3200]{2,1,0:T(8,128)}, bf16[2,1024,3200]{2,1,0:T(8,128)(2,1)},...) fusion(bf16[2,1024,3200]{2,1,0:T(8,128)(2,1)} %param.13, bf16[1,1024,3200]{2,1,0:T(8,128)(2,1)} %get-tuple-element.9, ...), kind=kLoop, calls=%fused_computation.20 | loop fusion | flops 249036800 | bytes 288358400 | tf_op jit(solution)/shard_map/convert_element_type | solution.py:30
  (19 shorter events, 0.1 us)
Async XLA Ops:
  7.2 758.3 %all-reduce.3.cloned.1.call-start = ((), (), s32[]{:S(2)}) async-start(), calls=%async_computation | async-start | bytes 78643200 | tf_op jit(solution)/shard_map/psum | solution.py:45
  16.8 48.3 %copy-start.6 = (f32[2048]{0:T(1024)}, f32[2048]{0:T(1024)S(1)}, u32[]{:S(2)}) copy-start(f32[2048]{0:T(1024)S(1)} %add_rsqrt_fusion) | copy-start | bytes 24580
  23.3 20.9 %copy-start.3 = (bf16[1,2048,1024]{2,1,0:T(8,128)(2,1)S(1)}, bf16[1,2048,1024]{2,1,0:T(8,128)(2,1)}, u32[]{:S(2)}) copy-start(bf16[1,2048,1024]{2,1,0:T(8,128)(2,1)} %param.11) | copy-start | bytes 12582916
  119.2 23.3 %copy-start.4 = (f32[2048]{0:T(1024)}, f32[2048]{0:T(1024)S(1)}, u32[]{:S(2)}) copy-start(f32[2048]{0:T(1024)S(1)} %get-tuple-element.26) | copy-start | bytes 24580
  181.5 22.6 %copy-start.2 = (bf16[2048,1024]{0,1:T(8,128)(2,1)S(1)}, bf16[2048,1024]{0,1:T(8,128)(2,1)}, u32[]{:S(2)}) copy-start(bf16[2048,1024]{0,1:T(8,128)(2,1)} %get-tuple-element.27) | copy-start | bytes 12582916
  275.3 22.8 %copy-start.5 = (f32[2048]{0:T(1024)S(1)}, f32[2048]{0:T(1024)}, u32[]{:S(2)}) copy-start(f32[2048]{0:T(1024)} %copy-done.4) | copy-start | bytes 24580
  275.3 22.8 %copy-start = (bf16[1,2048,1024]{1,2,0:T(8,128)(2,1)S(1)}, bf16[1,2048,1024]{1,2,0:T(8,128)(2,1)}, u32[]{:S(2)}) copy-start(bf16[1,2048,1024]{1,2,0:T(8,128)(2,1)} %copy.21) | copy-start | bytes 12582916
  325.8 21.2 %copy-start.1 = (bf16[1,2048,1024]{1,2,0:T(8,128)(2,1)S(1)}, bf16[1,2048,1024]{1,2,0:T(8,128)(2,1)}, u32[]{:S(2)}) copy-start(bf16[1,2048,1024]{1,2,0:T(8,128)(2,1)} %copy.20) | copy-start | bytes 12582916
  325.8 21.2 %copy-start.7 = (f32[2048]{0:T(1024)S(1)}, f32[2048]{0:T(1024)}, u32[]{:S(2)}) copy-start(f32[2048]{0:T(1024)} %copy-done.6) | copy-start | bytes 24580
Sparse Core Ops, SparseCore 0:
  401.0 364.4 all-reduce.2
where the time goes:
time: 921 us; the launch traced here: 914 us
  matrix products  371 us (40%)
  waiting for transfers between devices  365 us (40%)
  other arithmetic  151 us (16%)
  between operations  14.3 us (2%)
  local copies, waits for them, and re-layouts  13 us (1%)
    psum x1, waiting for transfers between devices, step(): summed[number] = [lax.psum(by_w[name], 'dp') for name in NAMES]  365 us
    convert_element_type x2, other arithmetic, adamw(): return ((w - 0.02 * step).astype(jnp.bfloat16), m, v)  141 us
    dot_general x5, matrix products, layer(): gate = jnp.dot(a, w['w_gate'], preferred_element_type=jnp.float32)  134 us
    dot_general x5, matrix products, layer(): up = jnp.dot(a, w['w_up'], preferred_element_type=jnp.float32)  127 us
    dot_general x5, matrix products, matmul(): jnp.dot(a, w, preferred_element_type=jnp.float32).astype(jnp.bfloat16)  111 us
  transfers between devices with their start and end apart: 1, of which 1 were waited for; matrix products, arithmetic and copies ran while one was open for 0% of the time, Pallas kernels for 0%

commit v1 on v0

v1 whole, which is shorter than its diff:
```python
import jax
import jax.numpy as jnp
from jax import lax
from jax.experimental import pallas as pl
from jax.experimental.pallas import tpu as pltpu
from jax.sharding import PartitionSpec as P

BF, F32 = jnp.bfloat16, jnp.float32
T, D, FF = 2048, 1024, 3200
FC = 640
NF = FF // FC
NC = 2 * NF
TB = 512
NT = T // TB
VMEM_LIMIT = 63 * 2**20

AXES = (1, 8, 4, 2)
ORDER = ((1, 8, 4, 2), (1, 4, 2, 8), (1, 2, 8, 4))


def dot(a, b, ca, cb):
    return lax.dot_general(a, b, (((ca,), (cb,)), ((), ())), preferred_element_type=F32)


def inverse_rms(wide):
    return lax.rsqrt(jnp.mean(wide * wide, -1, keepdims=True) + 1e-6)


def hidden_back(gate, up, by_hidden):
    s = 1.0 / (1.0 + jnp.exp(-gate))
    silu = gate * s
    hidden = (silu * up).astype(BF)
    by_gate = (by_hidden * up * (s + silu * (1.0 - s))).astype(BF)
    by_up = (by_hidden * silu).astype(BF)
    return hidden, by_gate, by_up


def any_spec(n):
    return [pl.BlockSpec(memory_space=pl.ANY)] * n


def forward_kernel(x_ref, wg, wu, wd, gu0, h1_ref, a1_ref, a1t_ref, a0t_ref, wgu, wdv, hid, gub, wsem, dsem, osem):
    i = pl.program_id(0)

    def weights(c):
        cols = pl.ds(pl.multiple_of(c * FC, 128), FC)
        return (
            pltpu.make_async_copy(wg.at[0, :, cols], wgu.at[c, :, pl.ds(0, FC)], wsem.at[c, 0]),
            pltpu.make_async_copy(wu.at[0, :, cols], wgu.at[c, :, pl.ds(FC, FC)], wsem.at[c, 1]),
        )

    down = pltpu.make_async_copy(wd.at[0], wdv, dsem)

    @pl.when(i == 0)
    def _():
        for c in range(NF):
            for copy in weights(c):
                copy.start()
        down.start()

    def out_copy(c, row_block):
        rows = pl.ds(pl.multiple_of(row_block * TB, TB), TB)
        return pltpu.make_async_copy(gub.at[lax.rem(c, 2)], gu0.at[c, rows, :], osem.at[lax.rem(c, 2)])

    wide = x_ref[...].astype(F32)
    a0 = (wide * inverse_rms(wide)).astype(BF)
    a0t_ref[...] = a0.T
    a1_ref[...] = a0

    def chunk(c, carry):
        @pl.when(i == 0)
        def _():
            for copy in weights(c):
                copy.wait()

        @pl.when(c >= 2)
        def _():
            out_copy(c, i).wait()

        gu = dot(a1_ref[...], wgu[c], 1, 0)
        gub[lax.rem(c, 2)] = gu
        gate = gu[:, :FC]
        hid[:, pl.ds(pl.multiple_of(c * FC, 128), FC)] = (gate * (1.0 / (1.0 + jnp.exp(-gate))) * gu[:, FC:]).astype(BF)
        out_copy(c, i).start()
        return carry

    lax.fori_loop(0, NF, chunk, 0)

    @pl.when(i == 0)
    def _():
        down.wait()

    h1 = (wide + dot(hid[...], wdv[...], 1, 0).astype(BF).astype(F32)).astype(BF)
    h1_ref[...] = h1
    wide1 = h1.astype(F32)
    a1 = (wide1 * inverse_rms(wide1)).astype(BF)
    a1_ref[...] = a1
    a1t_ref[...] = a1.T
    out_copy(NF - 2, i).wait()
    out_copy(NF - 1, i).wait()


def forward(x, wg, wu, wd):
    rows = pl.BlockSpec((TB, D), lambda i: (i, 0))
    columns = pl.BlockSpec((D, TB), lambda i: (0, i))
    return pl.pallas_call(
        forward_kernel,
        grid=(NT,),
        out_shape=[
            jax.ShapeDtypeStruct((NF, T, 2 * FC), F32),
            jax.ShapeDtypeStruct((T, D), BF),
            jax.ShapeDtypeStruct((T, D), BF),
            jax.ShapeDtypeStruct((D, T), BF),
            jax.ShapeDtypeStruct((D, T), BF),
        ],
        in_specs=[rows] + any_spec(3),
        out_specs=any_spec(1) + [rows, rows, columns, columns],
        scratch_shapes=[
            pltpu.VMEM((NF, D, 2 * FC), BF),
            pltpu.VMEM((FF, D), BF),
            pltpu.VMEM((TB, FF), BF),
            pltpu.VMEM((2, TB, 2 * FC), F32),
            pltpu.SemaphoreType.DMA((NF, 2)),
            pltpu.SemaphoreType.DMA,
            pltpu.SemaphoreType.DMA((2,)),
        ],
        compiler_params=pltpu.CompilerParams(dimension_semantics=("arbitrary",), vmem_limit_bytes=VMEM_LIMIT),
        cost_estimate=pl.CostEstimate(flops=6 * T * D * FF, bytes_accessed=100 * 2**20, transcendentals=T * FF),
        name="forward",
    )(x, wg, wu, wd)


def at(x, m):
    return x if isinstance(x, int) else pl.multiple_of(x, m)


class Sum:
    def __init__(self, g, out, recv_gate_up, recv_down, recv_down_ici, send, recv, local, free):
        self.g, self.out = g, out
        self.recv_gate_up, self.recv_down, self.recv_down_ici = recv_gate_up, recv_down, recv_down_ici
        self.send, self.recv, self.local, self.free = send, recv, local, free
        self.me = lax.axis_index("dp")

    def bit(self, b):
        return lax.rem(self.me // b, 2)

    def peer(self, b):
        return self.me + b * (1 - 2 * self.bit(b))

    def barrier(self):
        barrier = pltpu.get_barrier_semaphore()
        for b in AXES:
            pl.semaphore_signal(barrier, inc=1, device_id={"dp": self.peer(b)})
        pl.semaphore_wait(barrier, len(AXES))

    def origin(self, p, level, other=False):
        row, column = 0, 0
        for k in range(level):
            h = self.bit(ORDER[p][k])
            if other and k == level - 1:
                h = 1 - h
            if p < 2:
                row = row + h * (D // 2 >> k)
            elif k == 0:
                row = row + h * (FC // 2)
            else:
                column = column + h * (D >> k)
        return row, column

    def shape(self, p, level):
        return (D >> level, FC) if p < 2 else (FC // 2, D >> (level - 1))

    def window(self, ref, origin, shape):
        return ref.at[pl.ds(at(origin[0], 64), shape[0]), pl.ds(at(origin[1], 128), shape[1])]

    def landing(self, p, k, slot):
        if p < 2:
            return self.recv_gate_up[p].at[slot, pl.ds(D - (D >> k), D // 2 >> k), :]
        if k == 0:
            return self.recv_down.at[slot]
        return self.recv_down_ici.at[slot, :, pl.ds(D - (D >> (k - 1)), D >> k)]

    def halve(self, p, c, k):
        slot = lax.rem(c, 2)
        return pltpu.make_async_remote_copy(
            src_ref=self.window(self.g[p].at[slot], self.origin(p, k + 1, other=True), self.shape(p, k + 1)),
            dst_ref=self.landing(p, k, slot),
            send_sem=self.send.at[slot, p, k],
            recv_sem=self.recv.at[slot, p, k],
            device_id={"dp": self.peer(ORDER[p][k])},
        )

    def place(self, p, c, origin, shape):
        layer, start = 1 - c // NF, lax.rem(c, NF) * FC
        if p < 2:
            return self.out[p].at[layer, pl.ds(at(origin[0], 64), shape[0]), pl.ds(pl.multiple_of(start, 128), FC)]
        return self.out[p].at[layer, pl.ds(pl.multiple_of(start + origin[0], 64), shape[0]), pl.ds(at(origin[1], 128), shape[1])]

    def gather(self, p, c, j):
        slot, level = lax.rem(c, 2), 4 - j
        origin, shape = self.origin(p, level), self.shape(p, level)
        there = self.place(p, c, origin, shape)
        return pltpu.make_async_remote_copy(
            src_ref=self.window(self.g[p].at[slot], origin, shape) if j == 0 else there,
            dst_ref=there,
            send_sem=self.send.at[slot, p, 4 + j],
            recv_sem=self.recv.at[slot, p, 4 + j],
            device_id={"dp": self.peer(ORDER[p][3 - j])},
        )

    def keep(self, p, c):
        slot = lax.rem(c, 2)
        origin, shape = self.origin(p, 4), self.shape(p, 4)
        return pltpu.make_async_copy(self.window(self.g[p].at[slot], origin, shape), self.place(p, c, origin, shape), self.local.at[slot, p])

    def add(self, p, c, k):
        slot = lax.rem(c, 2)
        level = min(k + 1, 4)
        (row, column), shape = self.origin(p, level, other=k < 4), self.shape(p, level)
        ref = self.g[p]
        if p < 2:

            def block(i, carry):
                here = (slot, pl.ds(pl.multiple_of(row + i * 64, 64), 64), slice(None))
                total = ref[here].astype(F32)
                for j in range(k):
                    there = D - (D >> j) + row - self.origin(p, j + 1)[0] + i * 64
                    total = total + self.recv_gate_up[p][slot, pl.ds(pl.multiple_of(there, 64), 64), :].astype(F32)
                ref[here] = total.astype(BF)
                return carry

            lax.fori_loop(0, shape[0] // 64, block, 0)
        else:

            def block(i, carry):
                here = (slot, pl.ds(pl.multiple_of(row, 64), shape[0]), pl.ds(pl.multiple_of(column + i * 128, 128), 128))
                total = ref[here].astype(F32)
                for j in range(k):
                    there = column - self.origin(p, j + 1)[1] + i * 128
                    if j == 0:
                        total = total + self.recv_down[slot, :, pl.ds(pl.multiple_of(there, 128), 128)].astype(F32)
                    else:
                        there = there + D - (D >> (j - 1))
                        total = total + self.recv_down_ici[slot, :, pl.ds(pl.multiple_of(there, 128), 128)].astype(F32)
                ref[here] = total.astype(BF)
                return carry

            lax.fori_loop(0, shape[1] // 128, block, 0)

    def step(self, k, parts, c):
        if k == 0:

            @pl.when(jnp.logical_and(c >= 2, min(parts) == 0))
            def _():
                pl.semaphore_wait(self.free.at[0], 1)

        if k == 1:

            @pl.when(c >= 2)
            def _():
                for q in range(1, 4):
                    pl.semaphore_wait(self.free.at[q], 1)

        for p in parts:
            if 1 <= k <= 4:
                self.halve(p, c, k - 1).wait()
                self.add(p, c, k)
            if k < 4:
                self.halve(p, c, k).start()
            if k == 4:
                self.keep(p, c).start()
            if k == 5:
                self.keep(p, c).wait()
            if k >= 5:
                self.gather(p, c, k - 5).wait()
            if 4 <= k < 8:
                self.gather(p, c, k - 4).start()
        if k == 4:

            @pl.when(c < NC - 2)
            def _():
                for q, b in enumerate(AXES):
                    pl.semaphore_signal(self.free.at[q], inc=1, device_id={"dp": self.peer(b)})


AFTER = {
    2: ((2, 1), (7, 2)),
    4: ((3, 1),),
    5: ((4, 1), (8, 2)),
    6: ((5, 1), (0, 0)),
    7: ((6, 1), (1, 0)),
}


def backward_kernel(
    a1, a1t, a0t, dy, h1, gu0, wg, wu, wd,
    out_gate, out_up, out_down,
    a, at_, by_h, by_a, wgu, wdv, hid, dgu, g_gate, g_up, g_down, recv_gate, recv_up, recv_down, recv_down_ici,
    load_sem, w_sem, gu_sem, send, recv, local, free,
):
    total = Sum((g_gate, g_up, g_down), (out_gate, out_up, out_down), (recv_gate, recv_up), recv_down, recv_down_ici, send, recv, local, free)

    def weights(c, both):
        layer, start, slot = 1 - c // NF, lax.rem(c, NF) * FC, lax.rem(c, 2)
        columns = pl.ds(pl.multiple_of(start, 128), FC)
        copies = [pltpu.make_async_copy(wd.at[layer, pl.ds(pl.multiple_of(start, 64), FC), :], wdv.at[slot], w_sem.at[slot, 0])]
        if both:
            copies.append(pltpu.make_async_copy(wg.at[layer, :, columns], wgu.at[slot, :, pl.ds(0, FC)], w_sem.at[slot, 1]))
            copies.append(pltpu.make_async_copy(wu.at[layer, :, columns], wgu.at[slot, :, pl.ds(FC, FC)], w_sem.at[slot, 2]))
        return copies

    def kept(n):
        slot, c, t = lax.rem(n, 2), n // NT, lax.rem(n, NT)
        rows = pl.ds(pl.multiple_of(t * TB, TB), TB)
        return [
            pltpu.make_async_copy(
                gu0.at[c, rows, pl.ds(half * FC, FC)],
                by_a.at[pl.ds(pl.multiple_of((2 * slot + half) * TB, TB), TB), pl.ds(0, FC)],
                gu_sem.at[slot, half],
            )
            for half in range(2)
        ]

    load_dy = pltpu.make_async_copy(dy, by_h, load_sem.at[0])
    load_a = pltpu.make_async_copy(a1, a, load_sem.at[1])
    load_at = pltpu.make_async_copy(a1t, at_, load_sem.at[2])
    load_h1 = pltpu.make_async_copy(h1, a, load_sem.at[1])
    load_a0t = pltpu.make_async_copy(a0t, at_, load_sem.at[2])

    load_dy.start()
    load_a.start()
    for copy in weights(0, True):
        copy.start()
    load_at.start()
    by_a[...] = jnp.zeros_like(by_a)
    total.barrier()

    def sends(step, c):
        for k, back in AFTER.get(step, ()):
            if back == 0:
                total.step(k, (0, 1, 2), c)
            else:

                @pl.when(c >= back)
                def _(k=k, back=back):
                    total.step(k, (0, 1, 2), c - back)

    def rows_of(t):
        return pl.ds(pl.multiple_of(t * TB, TB), TB)

    def weight_gradients(c):
        slot = lax.rem(c, 2)
        g_down[slot] = dot(hid[...], by_h[...], 0, 0).astype(BF)
        sends(4, c)

        def block(m, carry):
            rows = pl.ds(pl.multiple_of(m * 512, 512), 512)
            both = dot(at_[rows, :], dgu[...], 1, 0).astype(BF)
            g_gate[slot, rows, :] = both[:, :FC]
            g_up[slot, rows, :] = both[:, FC:]

            @pl.when(m == 0)
            def _():
                sends(5, c)

            @pl.when(m == 1)
            def _():
                sends(6, c)

            return carry

        lax.fori_loop(0, 2, block, 0)

    def last_layer(c, carry):
        slot = lax.rem(c, 2)
        for copy in weights(c, True):
            copy.wait()

        @pl.when(c < NF - 1)
        def _():
            for copy in weights(c + 1, True):
                copy.start()

        @pl.when(c == NF - 1)
        def _():
            for copy in weights(c + 1, False):
                copy.start()

        @pl.when(c == 0)
        def _():
            load_dy.wait()
            load_a.wait()

        def block(t, carry):
            rows = rows_of(t)
            gu = dot(a[rows, :], wgu[slot], 1, 0)
            by_hidden = dot(by_h[rows, :], wdv[slot], 1, 1).astype(BF).astype(F32)
            hid[rows, :], dgu[rows, :FC], dgu[rows, FC:] = hidden_back(gu[:, :FC], gu[:, FC:], by_hidden)
            for n in range(NT):
                if n in AFTER:

                    @pl.when(t == n)
                    def _(n=n):
                        sends(n, c)

            return carry

        lax.fori_loop(0, NT, block, 0)

        @pl.when(c == 0)
        def _():
            load_at.wait()

        @pl.when(c == NF - 1)
        def _():
            load_h1.start()

        weight_gradients(c)

        @pl.when(c == NF - 1)
        def _():
            load_a0t.start()

        def input_block(t, carry):
            rows = rows_of(t)
            by_a[rows, :] += dot(dgu[rows, :], wgu[slot], 1, 1)

            @pl.when(t == 1)
            def _():
                sends(7, c)

            @pl.when(t == 3)
            def _():
                sends(8, c)

            return carry

        lax.fori_loop(0, NT, input_block, 0)
        return carry

    lax.fori_loop(0, NF, last_layer, 0)

    load_h1.wait()

    def norm_block(t, carry):
        rows = pl.ds(pl.multiple_of(t * 128, 128), 128)
        wide = a[rows, :].astype(F32)
        scale = inverse_rms(wide)
        by_normed = by_a[rows, :].astype(BF).astype(F32)
        through = by_normed * scale - wide * (scale * scale * scale * jnp.mean(by_normed * wide, -1, keepdims=True))
        by_h[rows, :] = (by_h[rows, :].astype(F32) + through.astype(BF).astype(F32)).astype(BF)
        return carry

    lax.fori_loop(0, T // 128, norm_block, 0)
    for copy in kept(0):
        copy.start()
    load_a0t.wait()

    def first_layer(c, carry):
        slot = lax.rem(c, 2)
        for copy in weights(c, False):
            copy.wait()

        @pl.when(c < NC - 1)
        def _():
            for copy in weights(c + 1, False):
                copy.start()

        def block(t, carry):
            rows = rows_of(t)
            n = (c - NF) * NT + t
            for copy in kept(n):
                copy.wait()

            @pl.when(n + 1 < NF * NT)
            def _():
                for copy in kept(n + 1):
                    copy.start()

            here = lax.rem(n, 2) * 2 * TB
            gate = by_a[pl.ds(pl.multiple_of(here, TB), TB), :FC]
            up = by_a[pl.ds(pl.multiple_of(here + TB, TB), TB), :FC]
            by_hidden = dot(by_h[rows, :], wdv[slot], 1, 1).astype(BF).astype(F32)
            hid[rows, :], dgu[rows, :FC], dgu[rows, FC:] = hidden_back(gate, up, by_hidden)
            for n in range(NT):
                if n in AFTER:

                    @pl.when(t == n)
                    def _(n=n):
                        sends(n, c)

            return carry

        lax.fori_loop(0, NT, block, 0)
        weight_gradients(c)
        sends(7, c)
        sends(8, c)
        return carry

    lax.fori_loop(NF, NC, first_layer, 0)
    for i in (NC, NC + 1):
        for step in range(9):
            for k, back in AFTER.get(step, ()):
                if i - back < NC:
                    total.step(k, (0, 1, 2), i - back)


def backward(a1, a1t, a0t, dy, h1, gu0, wg, wu, wd):
    dma = pltpu.SemaphoreType.DMA
    return pl.pallas_call(
        backward_kernel,
        out_shape=[jax.ShapeDtypeStruct((2, D, FF), BF), jax.ShapeDtypeStruct((2, D, FF), BF), jax.ShapeDtypeStruct((2, FF, D), BF)],
        in_specs=any_spec(9),
        out_specs=any_spec(3),
        scratch_shapes=[
            pltpu.VMEM((T, D), BF),
            pltpu.VMEM((D, T), BF),
            pltpu.VMEM((T, D), BF),
            pltpu.VMEM((T, D), F32),
            pltpu.VMEM((2, D, 2 * FC), BF),
            pltpu.VMEM((2, FC, D), BF),
            pltpu.VMEM((T, FC), BF),
            pltpu.VMEM((T, 2 * FC), BF),
            pltpu.VMEM((2, D, FC), BF),
            pltpu.VMEM((2, D, FC), BF),
            pltpu.VMEM((2, FC, D), BF),
            pltpu.VMEM((2, D - D // 16, FC), BF),
            pltpu.VMEM((2, D - D // 16, FC), BF),
            pltpu.VMEM((2, FC // 2, D), BF),
            pltpu.VMEM((2, FC // 2, D - D // 8), BF),
            dma((3,)),
            dma((2, 3)),
            dma((2, 2)),
            dma((2, 3, 8)),
            dma((2, 3, 8)),
            dma((2, 3)),
            pltpu.SemaphoreType.REGULAR((4,)),
        ],
        compiler_params=pltpu.CompilerParams(collective_id=0, has_side_effects=True, vmem_limit_bytes=VMEM_LIMIT),
        cost_estimate=pl.CostEstimate(flops=24 * T * D * FF, bytes_accessed=200 * 2**20, transcendentals=2 * T * FF),
        name="backward",
    )(a1, a1t, a0t, dy, h1, gu0, wg, wu, wd)


def adamw(w, m, v, g):
    m = 0.9 * m + 0.1 * g
    v = 0.95 * v + 0.05 * g * g
    step = m * lax.rsqrt(v + 1e-8) + 0.1 * w
    return (w - 0.02 * step).astype(BF), m, v


def solution(mesh):
    def step(x, dy, *arrays):
        weights, m, v = (arrays[i : i + 3] for i in (0, 3, 6))
        gu0, h1, a1, a1t, a0t = forward(x[0], *weights)
        gradients = backward(a1, a1t, a0t, dy[0], h1, gu0, *weights)
        new = [adamw(w.astype(F32), m, v, g.astype(F32)) for w, m, v, g in zip(weights, m, v, gradients, strict=True)]
        return tuple(one[which] for which in range(3) for one in new)

    return jax.shard_map(
        step,
        mesh=mesh,
        in_specs=(P(("rep", "dp"), None, None),) * 2 + (P(None, None, None),) * 9,
        out_specs=(P("rep", None, None),) * 9,
        check_vma=False,
    )
```

time: 921 us -> 564 us (0.61)
  Pallas kernels: 0 us -> 420 us
  matrix products: 371 us -> 0 us
  waiting for transfers between devices: 365 us -> 0 us
  between operations: 14.3 us -> 0.66 us
  local copies, waits for them, and re-layouts: 13 us -> 0 us
    pallas_call x0 -> x2, Pallas kernels: none -> 420 us  [the longest x1 364 us: backward(): pl.pallas_call(backward_kernel, out_shape=[jax.ShapeDtypeStruct((2, D, FF...]
    dot_general x15 -> x0, matrix products: 371 us -> none  [the longest x5 134 us: layer(): gate = jnp.dot(a, w['w_gate'], preferred_element_type=jnp.float32)]
    psum x1 -> x0, waiting for transfers between devices: 365 us -> none  [step(): summed[number] = [lax.psum(by_w[name], 'dp') for name in NAMES]]
    unnamed x18 -> x0, local copies, waits for them, and re-layouts: 13 us -> none
  transfers between devices with their start and end apart: 1 -> 0, of which waited for: 1 -> 0; matrix products, arithmetic and copies ran while one was open for 0% -> 0% of each run, Pallas kernels for 0% -> 0%
where the time goes in v1:
time: 564 us; the launch traced here: 563 us
  Pallas kernels  420 us (74%)
  other arithmetic  143 us (25%)
    pallas_call x1, Pallas kernels, backward(): pl.pallas_call(backward_kernel, out_shape=[jax.ShapeDtypeStruct((2, D, FF...  364 us
    convert_element_type x2, other arithmetic, adamw(): return ((w - 0.02 * step).astype(BF), m, v)  143 us
    pallas_call x1, Pallas kernels, forward(): pl.pallas_call(forward_kernel, grid=(NT,), out_shape=[jax.ShapeDtypeStruc...  56.1 us

profile of v1, /device:TPU:0, one launch (start us, length us, event | category | flops | bytes accessed | tf_op | source)
XLA Modules:
  0.0 563.2 jit_solution(4155253113769419944)
XLA Ops:
  0.6 56.1 %forward.1 = (f32[5,2048,1280]{2,1,0:T(8,128)}, bf16[2048,1024]{1,0:T(8,128)(2,1)}, bf16[2048,1024]{1,0:T(8,128)(2,1)}, bf16[1024,2048]{1,0:T(8,128)(2,1)}, bf16[1024,2048]{1,0:T(8,128)(2,1)}) custom-call(bf16[2048,1024]{1,0:T(8,128)(2,1)} %bitcast.2, bf16[2,1024,3200]{2,1,0:T(8,128)(2,1)} %wg.3, bf16[2,1024,3200]{2,1,0:T(8,128)(2,1)} %wu.3, ...), custom_call_target="tpu_custom_call" | custom-call | flops 40265318400 | bytes 104857600 | tf_op jit(solution)/shard_map/forward/pallas_call | solution.py:106
  56.7 363.7 %backward.1 = (bf16[2,1024,3200]{2,1,0:T(8,128)(2,1)}, bf16[2,1024,3200]{2,1,0:T(8,128)(2,1)}, bf16[2,3200,1024]{2,1,0:T(8,128)(2,1)}) custom-call(bf16[2048,1024]{1,0:T(8,128)(2,1)} %get-tuple-element.17.a1, bf16[1024,2048]{1,0:T(8,128)(2,1)} %get-tuple-element.18.a1t, bf16[1024,2048]{1,0:T(8,128)(2,1)} %get-tuple-element.19.a0t, ...), custom_call_target="tpu_custom_call" | custom-call | flops 161061273600 | bytes 209715200 | tf_op jit(solution)/shard_map/backward/pallas_call | solution.py:510
  420.5 93.3 %fusion.2 = (bf16[2,1024,3200]{2,1,0:T(8,128)(2,1)}, f32[2,1024,3200]{2,1,0:T(8,128)}, f32[2,1024,3200]{2,1,0:T(8,128)}, bf16[2,1024,3200]{2,1,0:T(8,128)(2,1)},...) fusion(bf16[2,1024,3200]{2,1,0:T(8,128)(2,1)} %wg.3, bf16[2,1024,3200]{2,1,0:T(8,128)(2,1)} %get-tuple-element.22, ...), kind=kLoop, calls=%fused_computation.14 | loop fusion | flops 209715200 | bytes 288358400 | tf_op jit(solution)/shard_map/convert_element_type | solution.py:549
  513.8 49.4 %fusion.10 = (bf16[2,3200,1024]{2,1,0:T(8,128)(2,1)}, f32[2,3200,1024]{2,1,0:T(8,128)}, f32[2,3200,1024]{2,1,0:T(8,128)}) fusion(bf16[2,3200,1024]{2,1,0:T(8,128)(2,1)} %wd.3, bf16[2,3200,1024]{2,1,0:T(8,128)(2,1)} %get-tuple-element.24, f32[2,3200,1024]{2,1,0:T(8,128)} %param.21, f32[2,3200,1024]{2,1,0:T(8,128)} %param.18), kind=kLoop, calls=%fused_computation.22 | loop fusion | flops 104857600 | bytes 144179200 | tf_op jit(solution)/shard_map/convert_element_type | solution.py:549

commit v2 on v1

v2 whole, which is shorter than its diff:
```python
import jax
import jax.numpy as jnp
from jax import lax
from jax.experimental import pallas as pl
from jax.experimental.pallas import tpu as pltpu
from jax.sharding import PartitionSpec as P

BF, F32 = jnp.bfloat16, jnp.float32
T, D, FF = 2048, 1024, 3200
FC = 640
NF = FF // FC
NC = 2 * NF
TB = 512
NT = T // TB
NG = NF + 1
NK = NC - NG
RS = 2
VMEM_LIMIT = 63 * 2**20

AXES = (1, 8, 4, 2)
ORDER = (AXES, (1, 4, 2, 8), (1, 2, 8, 4))


def dot(a, b, ca, cb):
    return lax.dot_general(a, b, (((ca,), (cb,)), ((), ())), preferred_element_type=F32)


def inverse_rms(wide):
    return lax.rsqrt(jnp.mean(wide * wide, -1, keepdims=True) + 1e-6)


def gated(gate, up):
    s = 1.0 / (1.0 + jnp.exp(-gate))
    silu = gate * s
    return (silu * up).astype(BF), up * (s + silu * (1.0 - s)), silu


def split(a, b):
    return (a // b, a % b) if isinstance(a, int) else (lax.div(a, jnp.int32(b)), lax.rem(a, jnp.int32(b)))


def layer_and_start(c):
    before, chunk = split(c, NF)
    return 1 - before, chunk * FC


def any_spec(n):
    return [pl.BlockSpec(memory_space=pl.ANY)] * n


def forward_kernel(x_ref, wg, wu, wd, by0, hid0, h1_ref, a1_ref, a0_ref, wgu, wdv, hid, byb, wsem, dsem, osem, hsem):
    i = pl.program_id(0)
    rows = pl.ds(pl.multiple_of(i * TB, TB), TB)

    def columns(c):
        return pl.ds(pl.multiple_of(c * FC, 128), FC)

    def weights(c):
        return (
            pltpu.make_async_copy(wg.at[0, :, columns(c)], wgu.at[c, :, pl.ds(0, FC)], wsem.at[c, 0]),
            pltpu.make_async_copy(wu.at[0, :, columns(c)], wgu.at[c, :, pl.ds(FC, FC)], wsem.at[c, 1]),
        )

    down = pltpu.make_async_copy(wd.at[0], wdv, dsem)

    @pl.when(i == 0)
    def _():
        for c in range(NF):
            for copy in weights(c):
                copy.start()
        down.start()

    def out_by(c):
        return pltpu.make_async_copy(byb.at[lax.rem(c, 2)], by0.at[c, rows, :], osem.at[lax.rem(c, 2)])

    def out_hid(c):
        return pltpu.make_async_copy(hid.at[:, columns(c)], hid0.at[c, rows, :], hsem.at[c])

    wide = x_ref[...].astype(F32)
    a0_ref[...] = (wide * inverse_rms(wide)).astype(BF)

    def chunk(c, carry):
        @pl.when(i == 0)
        def _():
            for copy in weights(c):
                copy.wait()

        @pl.when(c >= 2)
        def _():
            out_by(c).wait()

        gu = dot(a0_ref[...], wgu[c], 1, 0)
        hid[:, columns(c)], byb[lax.rem(c, 2), :, :FC], byb[lax.rem(c, 2), :, FC:] = gated(gu[:, :FC], gu[:, FC:])
        out_by(c).start()
        out_hid(c).start()
        return carry

    lax.fori_loop(0, NF, chunk, 0)

    @pl.when(i == 0)
    def _():
        down.wait()

    h1_ref[...] = (x_ref[...].astype(F32) + dot(hid[...], wdv[...], 1, 0).astype(BF).astype(F32)).astype(BF)
    wide1 = h1_ref[...].astype(F32)
    a1_ref[...] = (wide1 * inverse_rms(wide1)).astype(BF)
    for c in range(NF):
        out_hid(c).wait()
    out_by(NF - 2).wait()
    out_by(NF - 1).wait()


def forward(x, wg, wu, wd):
    rows = pl.BlockSpec((TB, D), lambda i: (i, 0))
    dma = pltpu.SemaphoreType.DMA
    return pl.pallas_call(
        forward_kernel,
        grid=(NT,),
        out_shape=[
            jax.ShapeDtypeStruct((NF, T, 2 * FC), F32),
            jax.ShapeDtypeStruct((NF, T, FC), BF),
            jax.ShapeDtypeStruct((T, D), BF),
            jax.ShapeDtypeStruct((T, D), BF),
            jax.ShapeDtypeStruct((T, D), BF),
        ],
        in_specs=[rows] + any_spec(3),
        out_specs=any_spec(2) + [rows] * 3,
        scratch_shapes=[
            pltpu.VMEM((NF, D, 2 * FC), BF),
            pltpu.VMEM((FF, D), BF),
            pltpu.VMEM((TB, FF), BF),
            pltpu.VMEM((2, TB, 2 * FC), F32),
            dma((NF, 2)),
            dma,
            dma((2,)),
            dma((NF,)),
        ],
        compiler_params=pltpu.CompilerParams(dimension_semantics=("arbitrary",), vmem_limit_bytes=VMEM_LIMIT),
        cost_estimate=pl.CostEstimate(flops=6 * T * D * FF, bytes_accessed=110 * 2**20, transcendentals=T * FF),
        name="forward",
    )(x, wg, wu, wd)


def at(x, m):
    return x if isinstance(x, int) else pl.multiple_of(x, m)


class Sum:
    def __init__(self, g, out, pieces, recv_gate_up, recv_down, recv_down_ici, send, recv, gather_send, gather_recv, local, free):
        self.g, self.out, self.pieces = g, out, pieces
        self.recv_gate_up, self.recv_down, self.recv_down_ici = recv_gate_up, recv_down, recv_down_ici
        self.send, self.recv, self.local, self.free = send, recv, local, free
        self.gather_send, self.gather_recv = gather_send, gather_recv
        me = lax.axis_index("dp")
        bits = {b: split(split(me, b)[0], 2)[1] for b in AXES}
        self.core = bits[1]
        self.peers = {b: me + b * (1 - 2 * bits[b]) for b in AXES}
        self.origins = {}
        for p in range(3):
            row = column = 0
            self.origins[p, 0, False] = row, column
            for k, b in enumerate(ORDER[p]):
                for other in (True, False):
                    h = 1 - bits[b] if other else bits[b]
                    if p < 2:
                        here = row + h * (D // 2 >> k), column
                    elif k == 0:
                        here = row + h * (FC // 2), column
                    else:
                        here = row, column + h * (D >> k)
                    self.origins[p, k + 1, other] = here
                row, column = here

    def peer(self, b):
        return self.peers[b]

    def arrive(self):
        for b in AXES:
            pl.semaphore_signal(pltpu.get_barrier_semaphore(), inc=1, device_id={"dp": self.peer(b)})

    def meet(self):
        pl.semaphore_wait(pltpu.get_barrier_semaphore(), len(AXES))

    def origin(self, p, level, other=False):
        return self.origins[p, level, other]

    def shape(self, p, level):
        return (D >> level, FC) if p < 2 else (FC // 2, D >> (level - 1))

    def window(self, ref, origin, shape):
        return ref.at[pl.ds(at(origin[0], 64), shape[0]), pl.ds(at(origin[1], 128), shape[1])]

    def landing(self, p, k, slot):
        if p < 2:
            return self.recv_gate_up[p].at[slot, pl.ds(D - (D >> k), D // 2 >> k), :]
        if k == 0:
            return self.recv_down.at[slot]
        return self.recv_down_ici.at[slot, :, pl.ds(D - (D >> (k - 1)), D >> k)]

    def halve(self, p, c, k):
        slot = lax.rem(c, RS)
        return pltpu.make_async_remote_copy(
            src_ref=self.window(self.g[p].at[slot], self.origin(p, k + 1, other=True), self.shape(p, k + 1)),
            dst_ref=self.landing(p, k, slot),
            send_sem=self.send.at[slot, p, k],
            recv_sem=self.recv.at[slot, p, k],
            device_id={"dp": self.peer(ORDER[p][k])},
        )

    def place(self, p, c, origin, shape):
        layer, start = layer_and_start(c)
        if p < 2:
            return self.out[p].at[layer, pl.ds(at(origin[0], 64), shape[0]), pl.ds(pl.multiple_of(start, 128), FC)]
        return self.out[p].at[layer, pl.ds(pl.multiple_of(start + origin[0], 16), shape[0]), pl.ds(at(origin[1], 128), shape[1])]

    def gather(self, p, c, j, q=0):
        slot, level = lax.rem(c, RS), 4 - j
        (row, column), (rows, columns) = self.origin(p, level), self.shape(p, level)
        if j == 2:
            rows = rows // 4
            row = row + q * rows
        there = self.place(p, c, (row, column), (rows, columns))
        return pltpu.make_async_remote_copy(
            src_ref=self.window(self.g[p].at[slot], (row, column), (rows, columns)) if j == 0 else there,
            dst_ref=there,
            send_sem=self.gather_send.at[c, p, 3 + q if q else j],
            recv_sem=self.gather_recv.at[c, p, 3 + q if q else j],
            device_id={"dp": self.peer(ORDER[p][3 - j])},
        )

    def keep(self, p, c, piece):
        slot = lax.rem(c, RS)
        origin, shape = self.origin(p, 4), self.shape(p, 4)
        own, sem = self.window(self.g[p].at[slot], origin, shape), self.local.at[slot, p]
        if not piece:
            return [pltpu.make_async_copy(own, self.place(p, c, origin, shape), sem)]
        there = self.pieces.at[c - NG, p]
        if p < 2:
            return [pltpu.make_async_copy(own, there, sem)]
        return [pltpu.make_async_copy(own.at[pl.ds(64 * b, 64), :], there.at[:, pl.ds(128 * b, 128)], sem) for b in range(5)]

    def kept(self, p, c):
        slot = lax.rem(c, RS)
        there = self.pieces.at[0, 0]
        return pltpu.make_async_copy(self.g[0].at[slot, pl.ds(0, D // 16), :], there, self.local.at[slot, p])

    def add(self, p, c, k):
        slot = lax.rem(c, RS)
        level = min(k + 1, 4)
        (row, column), shape = self.origin(p, level, other=k < 4), self.shape(p, level)
        ref = self.g[p]
        if p < 2:

            def block(i, carry):
                here = (slot, pl.ds(pl.multiple_of(row + i * 64, 64), 64), slice(None))
                total = ref[here].astype(F32)
                for j in range(k):
                    there = D - (D >> j) + row - self.origin(p, j + 1)[0] + i * 64
                    total = total + self.recv_gate_up[p][slot, pl.ds(pl.multiple_of(there, 64), 64), :].astype(F32)
                ref[here] = total.astype(BF)
                return carry

            lax.fori_loop(0, shape[0] // 64, block, 0)
        else:

            def block(i, carry):
                here = (slot, pl.ds(pl.multiple_of(row, 64), shape[0]), pl.ds(pl.multiple_of(column + i * 128, 128), 128))
                total = ref[here].astype(F32)
                for j in range(k):
                    there = column - self.origin(p, j + 1)[1] + i * 128
                    if j == 0:
                        total = total + self.recv_down[slot, :, pl.ds(pl.multiple_of(there, 128), 128)].astype(F32)
                    else:
                        there = there + D - (D >> (j - 1))
                        total = total + self.recv_down_ici[slot, :, pl.ds(pl.multiple_of(there, 128), 128)].astype(F32)
                ref[here] = total.astype(BF)
                return carry

            lax.fori_loop(0, shape[1] // 128, block, 0)

    def step(self, k, q, parts, c, piece):
        if k < 2:

            @pl.when(c >= RS)
            def _():
                for axis in range(1) if k == 0 else range(1, 4):
                    pl.semaphore_wait(self.free.at[axis, parts[0] // 2], 1)

        for p in parts:
            if 1 <= k <= 4:
                self.halve(p, c, k - 1).wait()
                self.add(p, c, k)
            if k < 4:
                self.halve(p, c, k).start()
            if k == 4:
                for copy in self.keep(p, c, piece):
                    copy.start()
            if k == 5:
                self.kept(p, c).wait()
            if k >= 5 and q == 0 and not piece:
                for quarter in range(4 if k == 7 else 1):
                    self.gather(p, c, k - 5, quarter).wait()
            if 4 <= k < 8 and not piece:
                self.gather(p, c, k - 4, q).start()
        if k == 4:

            @pl.when(c + RS < NC)
            def _():
                for axis, b in enumerate(AXES):
                    pl.semaphore_signal(self.free.at[axis, parts[0] // 2], inc=1, device_id={"dp": self.peer(b)})


STEPS = [(i, step) for i in range(NF) for step in range(9)] + [(i, step) for i in range(NF, NC + 8) for step in range(7)]

DIGITS = "0123456789abcdefghijklmnopqrstuvwxyzABCDEFGHIJKLMNOPQRSTUVWXYZ"
STAGES = [(k, q) for k in range(9) for q in range(4 if k == 6 else 1)]
TIMES = (
    ("57bdfimnovFK", "458cfimnpuHJ"),
    ("57bdfimnovEK", "458cfimnpuGI"),
    ("57bdfimnouEK", "458cfimnptGI"),
    ("57bdgimnuvAG", "459cegmouwFI"),
    ("568deiswwzDK", "458dejsuBBHL"),
    ("56bdfhttuvGK", "45acehpqstzH"),
    ("58cehi", "68cegh"),
    ("58cehi", "68cegh"),
    ("5agszA", "4aiqwC"),
    ("58cnxG", "46flDI"),
)


def plan():
    entries = {}
    for c, both in enumerate(TIMES):
        for parts, times in zip(((0, 1), (2,)), both, strict=True):
            for (k, q), digit in zip(STAGES, times):
                entries.setdefault(STEPS[STEPS.index((c, 0)) + DIGITS.index(digit)], []).append((k, q, parts, c))
    return entries


def first(entry):
    k, q, parts, *_ = entry
    return (k > 4, -k if k <= 4 else k, q, parts)


PLAN = plan()
LAST, FIRST = range(NF), range(NF, NC)


def backward_kernel(
    a1, a0, dy, h1, by0, hid0, wg, wu, wd,
    out_gate, out_up, out_down, pieces,
    a, by_h, by_a, wgu, wdv, hid, dgu, g_gate, g_up, g_down, recv_gate, recv_up, recv_down, recv_down_ici,
    rows_sem, load_sem, w_sem, by_sem, send, recv, gather_send, gather_recv, local, free,
):
    total = Sum(
        (g_gate, g_up, g_down), (out_gate, out_up, out_down), pieces,
        (recv_gate, recv_up), recv_down, recv_down_ici, send, recv, gather_send, gather_recv, local, free,
    )

    def weights(c, both):
        (layer, start), slot = layer_and_start(c), lax.rem(c, 2)
        columns = pl.ds(pl.multiple_of(start, 128), FC)
        copies = [pltpu.make_async_copy(wd.at[layer, pl.ds(pl.multiple_of(start, 64), FC), :], wdv.at[slot], w_sem.at[slot, 0])]
        if both:
            copies.append(pltpu.make_async_copy(wg.at[layer, :, columns], wgu.at[slot, :, pl.ds(0, FC)], w_sem.at[slot, 1]))
            copies.append(pltpu.make_async_copy(wu.at[layer, :, columns], wgu.at[slot, :, pl.ds(FC, FC)], w_sem.at[slot, 2]))
        return copies

    def rows_of(t):
        return pl.ds(pl.multiple_of(t * TB, TB), TB)

    def first_rows(t):
        return [
            pltpu.make_async_copy(dy.at[rows_of(t), :], by_h.at[rows_of(t), :], rows_sem.at[t, 0]),
            pltpu.make_async_copy(a1.at[rows_of(t), :], a.at[rows_of(t), :], rows_sem.at[t, 1]),
        ]

    def derivatives(c, t):
        return pltpu.make_async_copy(by0.at[c - NF, rows_of(t), :], by_a.at[rows_of(t), :], by_sem.at[t])

    def hidden(c):
        return pltpu.make_async_copy(hid0.at[c - NF], hid, load_sem.at[2])

    load_h1 = pltpu.make_async_copy(h1, a, load_sem.at[0])
    load_a0 = pltpu.make_async_copy(a0, a, load_sem.at[1])

    total.arrive()
    for copy in weights(0, True) + first_rows(0):
        copy.start()
    by_a[:, :D] = jnp.zeros((T, D), F32)
    total.meet()

    def sends(step, c, span):
        found = {}
        for i in span:
            for k, q, parts, chunk in PLAN.get((i, step), ()):
                found.setdefault((k, q, parts, i - chunk, chunk >= NG), []).append(i)
        runs = []
        for entry, chunks in sorted(found.items(), key=lambda e: first(e[0])):
            for low in (i for i in chunks if i - 1 not in chunks):
                high = next(i for i in chunks if i >= low and i + 1 not in chunks)
                same = [run for run in runs if run[:2] == [low, high]]
                if same and all(run[0] > high or run[1] < low for run in runs[runs.index(same[-1]) + 1 :]):
                    same[-1][2].append(entry)
                else:
                    runs.append([low, high, [entry]])
        for low, high, entries in runs:

            @pl.when(jnp.logical_and(c >= low, c <= high))
            def _(entries=entries):
                for k, q, parts, back, piece in entries:
                    total.step(k, q, parts, c - back, piece)

    def sends_of_block(t, c, span):
        for n in range(NT):

            @pl.when(t == n)
            def _(n=n):
                sends(n, c, span)

    def weight_gradients(c, span):
        slot = lax.rem(c, RS)
        g_down[slot] = dot(hid[...], by_h[...], 0, 0).astype(BF)

        @pl.when(jnp.logical_and(c >= NF - 1, c < NC - 1))
        def _():
            hidden(c + 1).start()

        sends(4, c, span)

        def block(m, carry):
            half = jnp.where(m == 0, 1 - total.core, total.core)
            rows = pl.ds(pl.multiple_of(half * (D // 2), D // 2), D // 2)
            both = dot(a[:, rows], dgu[...], 0, 0).astype(BF)
            g_gate[slot, rows, :] = both[:, :FC]
            g_up[slot, rows, :] = both[:, FC:]

            @pl.when(m == 0)
            def _():
                sends(5, c, span)

            @pl.when(m == 1)
            def _():
                sends(6, c, span)

            return carry

        lax.fori_loop(0, 2, block, 0)

    def input_rows(t, slot):
        rows = rows_of(t)
        by_a[rows, :D] += dot(dgu[rows, :], wgu[slot], 1, 1)

    def last_layer(c, carry):
        slot = lax.rem(c, 2)
        for copy in weights(c, True):
            copy.wait()

        @pl.when(jnp.logical_and(c > 0, c < NF - 1))
        def _():
            for copy in weights(c + 1, True):
                copy.start()

        @pl.when(c == NF - 1)
        def _():
            for copy in weights(c + 1, False):
                copy.start()

        def block(t, carry):
            @pl.when(c == 0)
            def _():
                for copy in first_rows(t):
                    copy.wait()

                @pl.when(t < NT - 1)
                def _():
                    for copy in first_rows(t + 1):
                        copy.start()

                @pl.when(t == NT - 1)
                def _():
                    for copy in weights(1, True):
                        copy.start()

            rows = rows_of(t)
            gu = dot(a[rows, :], wgu[slot], 1, 0)
            by_hidden = dot(by_h[rows, :], wdv[slot], 1, 1).astype(BF).astype(F32)
            hid[rows, :], by_gate, by_up = gated(gu[:, :FC], gu[:, FC:])
            dgu[rows, :FC] = (by_hidden * by_gate).astype(BF)
            dgu[rows, FC:] = (by_hidden * by_up).astype(BF)
            sends_of_block(t, c, LAST)
            return carry

        lax.fori_loop(0, NT, block, 0)

        weight_gradients(c, LAST)

        @pl.when(c == NF - 1)
        def _():
            load_h1.start()

        def input_block(t, carry):
            input_rows(t, slot)

            @pl.when(t == 1)
            def _():
                sends(7, c, LAST)

            @pl.when(t == 3)
            def _():
                sends(8, c, LAST)

            return carry

        lax.fori_loop(0, jnp.where(c < NF - 1, NT, 1), input_block, 0)
        return carry

    lax.fori_loop(0, NF, last_layer, 0)
    load_h1.wait()

    def norm_rows(t):
        for half in range(2):
            rows = pl.ds(pl.multiple_of(t * TB + half * (TB // 2), TB // 2), TB // 2)
            wide = a[rows, :].astype(F32)
            scale = inverse_rms(wide)
            by_normed = by_a[rows, :D].astype(BF).astype(F32)
            through = by_normed * scale - wide * (scale * scale * scale * jnp.mean(by_normed * wide, -1, keepdims=True))
            by_h[rows, :] = (by_h[rows, :].astype(F32) + through.astype(BF).astype(F32)).astype(BF)

    def norm_block(t, carry):
        norm_rows(t - 1)
        input_rows(t, (NF - 1) % 2)
        derivatives(NF, t - 1).start()

        @pl.when(t == 1)
        def _():
            sends(7, NF - 1, LAST[-1:])

        @pl.when(t == 3)
        def _():
            sends(8, NF - 1, LAST[-1:])

        return carry

    lax.fori_loop(1, NT, norm_block, 0)
    norm_rows(NT - 1)
    derivatives(NF, NT - 1).start()
    load_a0.start()

    def first_layer(c, carry):
        slot = lax.rem(c, 2)
        for copy in weights(c, False):
            copy.wait()

        @pl.when(c < NC - 1)
        def _():
            for copy in weights(c + 1, False):
                copy.start()

        def block(t, carry):
            rows = rows_of(t)
            derivatives(c, t).wait()
            by_hidden = dot(by_h[rows, :], wdv[slot], 1, 1).astype(BF).astype(F32)
            dgu[rows, :FC] = (by_hidden * by_a[rows, :FC]).astype(BF)
            dgu[rows, FC:] = (by_hidden * by_a[rows, FC:]).astype(BF)

            @pl.when(c < NC - 1)
            def _():
                derivatives(c + 1, t).start()

            sends_of_block(t, c, FIRST)
            return carry

        lax.fori_loop(0, NT, block, 0)
        hidden(c).wait()

        @pl.when(c == NF)
        def _():
            load_a0.wait()

        weight_gradients(c, FIRST)
        return carry

    lax.fori_loop(NF, NC, first_layer, 0)
    for (i, _), entries in sorted(PLAN.items()):
        if i >= NC:
            for k, q, parts, chunk in sorted(entries, key=first):
                total.step(k, q, parts, chunk, chunk >= NG)


def backward(a1, a0, dy, h1, by0, hid0, wg, wu, wd):
    dma = pltpu.SemaphoreType.DMA
    return pl.pallas_call(
        backward_kernel,
        out_shape=[jax.ShapeDtypeStruct(shape, BF) for shape in ((2, D, FF), (2, D, FF), (2, FF, D), (NK, 3, D // 16, FC))],
        in_specs=any_spec(9),
        out_specs=any_spec(4),
        scratch_shapes=[
            pltpu.VMEM((T, D), BF),
            pltpu.VMEM((T, D), BF),
            pltpu.VMEM((T, 2 * FC), F32),
            pltpu.VMEM((2, D, 2 * FC), BF),
            pltpu.VMEM((2, FC, D), BF),
            pltpu.VMEM((T, FC), BF),
            pltpu.VMEM((T, 2 * FC), BF),
            pltpu.VMEM((RS, D, FC), BF),
            pltpu.VMEM((RS, D, FC), BF),
            pltpu.VMEM((RS, FC, D), BF),
            pltpu.VMEM((RS, D - D // 16, FC), BF),
            pltpu.VMEM((RS, D - D // 16, FC), BF),
            pltpu.VMEM((RS, FC // 2, D), BF),
            pltpu.VMEM((RS, FC // 2, D - D // 8), BF),
            dma((NT, 2)),
            dma((3,)),
            dma((2, 3)),
            dma((NT,)),
            dma((RS, 3, 4)),
            dma((RS, 3, 4)),
            dma((NG, 3, 7)),
            dma((NG, 3, 7)),
            dma((RS, 3)),
            pltpu.SemaphoreType.REGULAR((4, 2)),
        ],
        compiler_params=pltpu.CompilerParams(collective_id=0, has_side_effects=True, vmem_limit_bytes=VMEM_LIMIT),
        cost_estimate=pl.CostEstimate(flops=24 * T * D * FF, bytes_accessed=200 * 2**20, transcendentals=2 * T * FF),
        name="backward",
    )(a1, a0, dy, h1, by0, hid0, wg, wu, wd)


SLOTS = 4
QUARTERS = ((D // 4, FC), (D // 4, FC), (FC // 4, D))


def adamw(w, m, v, g):
    m = 0.9 * m + 0.1 * g
    v = 0.95 * v + 0.05 * g * g
    step = m * lax.rsqrt(v + 1e-8) + 0.1 * w
    return (w - 0.02 * step).astype(BF), m, v


def owner(p, half, q):
    bits = ORDER[p]
    return half * bits[0] + q // 4 * bits[1] + q // 2 % 2 * bits[2] + q % 2 * bits[3]


def adamw_kernel(chunks, in_pieces, n_before, *refs):
    w, m, v = refs[0:3], refs[3:6], refs[6:9]
    n_g = 1 if in_pieces else 3
    g, outs = refs[9 : 9 + n_g], refs[9 + n_g + n_before : 18 + n_g + n_before]
    *bufs, load_sem, store_sem = refs[18 + n_g + n_before :]
    units = 4 * len(chunks)

    def window(ref, p, c, q):
        rows, columns = QUARTERS[p]
        layer, start = layer_and_start(c)
        if p < 2:
            return ref.at[layer, pl.ds(pl.multiple_of(q * rows, rows), rows), pl.ds(pl.multiple_of(start, 128), FC)]
        return ref.at[layer, pl.ds(pl.multiple_of(start + q * rows, 32), rows), :]

    def gradient(p, c, q, to, sem):
        if not in_pieces:
            return [pltpu.make_async_copy(window(g[p], p, c, q), to, sem)]
        half, low = split(q, 2)
        if p < 2:
            return [
                pltpu.make_async_copy(g[0].at[owner(p, half, e) + low * ORDER[p][1], c - NG, p], to.at[pl.ds(64 * e, 64), :], sem) for e in range(4)
            ]
        copies = []
        for e in range(8):
            piece, columns = g[0].at[owner(p, half, e), c - NG, p], pl.ds(128 * e, 128)
            for b, rows, src, dst in ((3 * low, 64, 0, 32 * low), (1 + 3 * low, 64, 0, 64 + 32 * low), (2, 32, 32 * low, 128 - 128 * low)):
                there = pl.ds(pl.multiple_of(128 * b, 128), 128)
                copies.append(
                    pltpu.make_async_copy(
                        piece.at[pl.ds(at(src, 32), rows), there], to.at[pl.ds(pl.multiple_of(dst, 32), rows), columns], sem
                    )
                )
        return copies

    def loads(n, act):
        (c, q), slot = split(n + 4 * chunks[0], 4), lax.rem(n, SLOTS)
        for p in range(3):
            for b, ref in enumerate((w[p], m[p], v[p])):
                copy = pltpu.make_async_copy(window(ref, p, c, q), bufs[4 * p + b].at[slot], load_sem.at[slot, p, b])
                copy.start() if act == "start" else copy.wait()
            to, sem = bufs[4 * p + 3].at[slot], load_sem.at[slot, p, 3]
            if act == "start":
                for copy in gradient(p, c, q, to, sem):
                    copy.start()
            else:
                pltpu.make_async_copy(window(w[p], p, c, q), to, sem).wait()

    def stores(n, act):
        (c, q), slot = split(n + 4 * chunks[0], 4), lax.rem(n, SLOTS)
        for p in range(3):
            for b in range(3):
                copy = pltpu.make_async_copy(bufs[4 * p + b].at[slot], window(outs[3 * b + p], p, c, q), store_sem.at[slot, p, b])
                copy.start() if act == "start" else copy.wait()

    loads(0, "start")
    loads(1, "start")

    def unit(n, carry):
        slot = lax.rem(n, SLOTS)

        @pl.when(n >= 2)
        def _():
            stores(n - 2, "wait")

        @pl.when(n + 2 < units)
        def _():
            loads(n + 2, "start")

        loads(n, "wait")
        for p in range(3):
            block = 64 if p < 2 else 32

            def rows_block(r, carry, buf=bufs[4 * p : 4 * p + 4], block=block):
                here = (slot, pl.ds(pl.multiple_of(r * block, block), block), slice(None))
                buf[0][here], buf[1][here], buf[2][here] = adamw(
                    buf[0][here].astype(F32), buf[1][here], buf[2][here], buf[3][here].astype(F32)
                )
                return carry

            lax.fori_loop(0, QUARTERS[p][0] // block, rows_block, 0)
        stores(n, "start")
        return carry

    lax.fori_loop(0, units, unit, 0)
    stores(units - 2, "wait")
    stores(units - 1, "wait")


def adamw_call(chunks, arrays, gradients, before=()):
    in_pieces, n_before = len(gradients) == 1, len(before)

    def kernel(*refs):
        adamw_kernel(chunks, in_pieces, n_before, *refs)

    elements, n_in = 3 * D * FC * len(chunks), 9 + len(gradients)
    return pl.pallas_call(
        kernel,
        out_shape=[jax.ShapeDtypeStruct(a.shape, a.dtype) for a in arrays],
        in_specs=any_spec(n_in + n_before),
        out_specs=any_spec(9),
        input_output_aliases={n_in + i: i for i in range(n_before)},
        scratch_shapes=[pltpu.VMEM((SLOTS, *shape), t) for shape in QUARTERS for t in (BF, F32, F32, BF)]
        + [pltpu.SemaphoreType.DMA((SLOTS, 3, 4)), pltpu.SemaphoreType.DMA((SLOTS, 3, 3))],
        compiler_params=pltpu.CompilerParams(vmem_limit_bytes=VMEM_LIMIT),
        cost_estimate=pl.CostEstimate(flops=15 * elements, bytes_accessed=22 * elements, transcendentals=elements),
        name="adamw_pieces" if in_pieces else "adamw_whole",
    )(*arrays, *gradients, *before)


def solution(mesh):
    def step(x, dy, *arrays):
        weights = arrays[:3]
        by0, hid0, h1, a1, a0 = forward(x[0], *weights)
        *gradients, pieces = backward(a1, a0, dy[0], h1, by0, hid0, *weights)
        gathered = lax.all_gather(pieces, "dp")
        new = adamw_call(range(NG), arrays, gradients)
        return tuple(adamw_call(range(NG, NC), arrays, (gathered,), new))

    return jax.shard_map(
        step,
        mesh=mesh,
        in_specs=(P(("rep", "dp"), None, None),) * 2 + (P(None, None, None),) * 9,
        out_specs=(P("rep", None, None),) * 9,
        check_vma=False,
    )
```

time: 564 us -> 467 us (0.83)
  other arithmetic: 143 us -> 0 us
  Pallas kernels: 420 us -> 452 us
  between operations: 0.66 us -> 14.1 us
    convert_element_type x2 -> x0, other arithmetic: 143 us -> none  [adamw(): return ((w - 0.02 * step).astype(BF), m, v)]
    pallas_call x1 -> x3, Pallas kernels: 364 us -> 396 us  [the longest x1 256 us: backward(): pl.pallas_call(backward_kernel, out_shape=[jax.ShapeDtypeStruct(shape, BF...]
  transfers between devices with their start and end apart: 0 -> 1, of which waited for: 0 -> 0; matrix products, arithmetic and copies ran while one was open for 0% -> 0% of each run, Pallas kernels for 0% -> 18%
where the time goes in v2:
time: 467 us
  Pallas kernels  452 us (97%)
  between operations  14.1 us (3%)
    pallas_call x1, Pallas kernels, backward(): pl.pallas_call(backward_kernel, out_shape=[jax.ShapeDtypeStruct(shape, BF...  256 us
    pallas_call x2, Pallas kernels, adamw_call(): pl.pallas_call(kernel, out_shape=[jax.ShapeDtypeStruct(a.shape, a.dtype)...  140 us
    pallas_call x1, Pallas kernels, forward(): pl.pallas_call(forward_kernel, grid=(NT,), out_shape=[jax.ShapeDtypeStruc...  56.3 us
  transfers between devices with their start and end apart: 1, of which 0 were waited for; matrix products, arithmetic and copies ran while one was open for 0% of the time, Pallas kernels for 18%

profile of v2, /device:TPU:0, one launch (start us, length us, event | category | flops | bytes accessed | tf_op | source)
XLA Modules:
  0.0 466.6 jit_solution(1338941161336472638)
XLA Ops:
  7.2 0.0 all-gather.3.cloned.1.call-start
  7.2 56.3 %forward.1 = (f32[5,2048,1280]{2,1,0:T(8,128)}, bf16[5,2048,640]{2,1,0:T(8,128)(2,1)}, bf16[2048,1024]{1,0:T(8,128)(2,1)}, bf16[2048,1024]{1,0:T(8,128)(2,1)}, bf16[2048,1024]{1,0:T(8,128)(2,1)}) custom-call(bf16[2048,1024]{1,0:T(8,128)(2,1)} %bitcast.4, bf16[2,1024,3200]{2,1,0:T(8,128)(2,1)} %refs_0_.3, bf16[2,1024,3200]{2,1,0:T(8,128)(2,1)} %refs_1_.3, ...), custom_call_target="tpu_custom_call" | custom-call | flops 40265318400 | bytes 115343360 | tf_op jit(solution)/shard_map/forward/pallas_call | solution.py:116
  63.6 256.5 %backward.1 = (bf16[2,1024,3200]{2,1,0:T(8,128)(2,1)}, bf16[2,1024,3200]{2,1,0:T(8,128)(2,1)}, bf16[2,3200,1024]{2,1,0:T(8,128)(2,1)}, bf16[4,3,64,640]{3,2,1,0:T(8,128)(2,1)}) custom-call(bf16[2048,1024]{1,0:T(8,128)(2,1)} %get-tuple-element.27.a1, bf16[2048,1024]{1,0:T(8,128)(2,1)} %get-tuple-element.28.a0, bf16[2048,1024]{1,0:T(8,128)(2,1)} %bitcast.5, ...), custom_call_target="tpu_custom_call" | custom-call | flops 161061273600 | bytes 209715200 | tf_op jit(solution)/shard_map/backward/pallas_call | solution.py:593
  320.1 0.0 all-gather.3.cloned.1.call-update
  320.1 83.3 %adamw_whole.1 = (bf16[2,1024,3200]{2,1,0:T(8,128)(2,1)}, bf16[2,1024,3200]{2,1,0:T(8,128)(2,1)}, bf16[2,3200,1024]{2,1,0:T(8,128)(2,1)}, f32[2,1024,3200]{2,1,0...) custom-call(bf16[2,1024,3200]{2,1,0:T(8,128)(2,1)} %refs_0_.3, ...), custom_call_target="tpu_custom_call" | custom-call | flops 176947200 | bytes 259522560 | tf_op jit(solution)/shard_map/adamw_whole/pallas_call | solution.py:741
  403.4 0.0 all-gather.3.cloned.1.call-done
  403.4 56.3 %adamw_pieces.1 = (bf16[2,1024,3200]{2,1,0:T(8,128)(2,1)}, bf16[2,1024,3200]{2,1,0:T(8,128)(2,1)}, bf16[2,3200,1024]{2,1,0:T(8,128)(2,1)}, f32[2,1024,3200]{2,1,...) custom-call(bf16[2,1024,3200]{2,1,0:T(8,128)(2,1)} %refs_0_.3, ...), custom_call_target="tpu_custom_call", output_to_operand_aliasing={{0}: (10, {}), {1}: (11, {}), {2}: (12, {}), {3}: (13, {}),... | custom-call | flops 117964800 | bytes 173015040 | tf_op jit(solution)/shard_map/adamw_pieces/pallas_call | solution.py:741
Async XLA Ops:
  7.2 396.3 %all-gather.3.cloned.1.call-start = ((), (), s32[]{:S(2)}) async-start(), calls=%async_computation | async-start | bytes 16711680 | tf_op jit(solution)/shard_map/all_gather | solution.py:760
Sparse Core Ops, SparseCore 0:
  320.2 71.9 all-gather.2

commit v3 on v2

--- a/solution.py
+++ b/solution.py
@@ -14,8 +14,9 @@
 NT = T // TB
 NG = NF + 1
 NK = NC - NG
+BETWEEN = -1
 RS = 2
-VMEM_LIMIT = 63 * 2**20
+VMEM_LIMIT = 63 << 20
 
 AXES = (1, 8, 4, 2)
 ORDER = (AXES, (1, 4, 2, 8), (1, 2, 8, 4))
@@ -136,7 +137,7 @@
             dma((NF,)),
         ],
         compiler_params=pltpu.CompilerParams(dimension_semantics=("arbitrary",), vmem_limit_bytes=VMEM_LIMIT),
-        cost_estimate=pl.CostEstimate(flops=6 * T * D * FF, bytes_accessed=110 * 2**20, transcendentals=T * FF),
+        cost_estimate=pl.CostEstimate(flops=6 * T * D * FF, bytes_accessed=110 << 20, transcendentals=T * FF),
         name="forward",
     )(x, wg, wu, wd)
 
@@ -279,12 +280,13 @@
             lax.fori_loop(0, shape[1] // 128, block, 0)
 
     def step(self, k, q, parts, c, piece):
+        group = parts[0] // 2
         if k < 2:
 
             @pl.when(c >= RS)
             def _():
                 for axis in range(1) if k == 0 else range(1, 4):
-                    pl.semaphore_wait(self.free.at[axis, parts[0] // 2], 1)
+                    pl.semaphore_wait(self.free.at[axis, group], 1)
 
         for p in parts:
             if 1 <= k <= 4:
@@ -307,24 +309,25 @@
             @pl.when(c + RS < NC)
             def _():
                 for axis, b in enumerate(AXES):
-                    pl.semaphore_signal(self.free.at[axis, parts[0] // 2], inc=1, device_id={"dp": self.peer(b)})
-
-
-STEPS = [(i, step) for i in range(NF) for step in range(9)] + [(i, step) for i in range(NF, NC + 8) for step in range(7)]
+                    pl.semaphore_signal(self.free.at[axis, group], inc=1, device_id={"dp": self.peer(b)})
+
+
+STEPS = [(i, step) for i in range(NF) for step in range(7)] + [(BETWEEN, step) for step in range(10)]
+STEPS += [(i, step) for i in range(NF, NC + 8) for step in range(7)]
 
 DIGITS = "0123456789abcdefghijklmnopqrstuvwxyzABCDEFGHIJKLMNOPQRSTUVWXYZ"
 STAGES = [(k, q) for k in range(9) for q in range(4 if k == 6 else 1)]
 TIMES = (
-    ("57bdfimnovFK", "458cfimnpuHJ"),
-    ("57bdfimnovEK", "458cfimnpuGI"),
-    ("57bdfimnouEK", "458cfimnptGI"),
-    ("57bdgimnuvAG", "459cegmouwFI"),
-    ("568deiswwzDK", "458dejsuBBHL"),
-    ("56bdfhttuvGK", "45acehpqstzH"),
-    ("58cehi", "68cegh"),
-    ("58cehi", "68cegh"),
-    ("5agszA", "4aiqwC"),
-    ("58cnxG", "46flDI"),
+    ("57bdgirDFJUX", "46acehkvvJRX"),
+    ("56adginrvBIM", "45acehrtvwJP"),
+    ("56adginrvAIM", "45acehrtvvJP"),
+    ("57bdgmootzBQ", "45adglnotOSX"),
+    ("57adekrtyJRW", "46aefgmstyOX"),
+    ("56bcfinrttCE", "46bcdhmsvxBH"),
+    ("56behi", "45adgh"),
+    ("58cegi", "48cegh"),
+    ("58gouA", "57gsxF"),
+    ("58bmCV", "47bmFW"),
 )
 
 
@@ -348,23 +351,25 @@
 
 def backward_kernel(
     a1, a0, dy, h1, by0, hid0, wg, wu, wd,
-    out_gate, out_up, out_down, pieces,
+    out_gate, out_up, out_down, pieces, kept_dgu,
     a, by_h, by_a, wgu, wdv, hid, dgu, g_gate, g_up, g_down, recv_gate, recv_up, recv_down, recv_down_ici,
-    rows_sem, load_sem, w_sem, by_sem, send, recv, gather_send, gather_recv, local, free,
+    rows_sem, load_sem, w_sem, by_sem, dgu_sem, send, recv, gather_send, gather_recv, local, free,
 ):
     total = Sum(
         (g_gate, g_up, g_down), (out_gate, out_up, out_down), pieces,
         (recv_gate, recv_up), recv_down, recv_down_ici, send, recv, gather_send, gather_recv, local, free,
     )
 
-    def weights(c, both):
+    def down_weights(c):
+        (layer, start), slot = layer_and_start(c), lax.rem(c, 2)
+        return [pltpu.make_async_copy(wd.at[layer, pl.ds(pl.multiple_of(start, 64), FC), :], wdv.at[slot], w_sem.at[slot, 2])]
+
+    def input_weights(c):
         (layer, start), slot = layer_and_start(c), lax.rem(c, 2)
         columns = pl.ds(pl.multiple_of(start, 128), FC)
-        copies = [pltpu.make_async_copy(wd.at[layer, pl.ds(pl.multiple_of(start, 64), FC), :], wdv.at[slot], w_sem.at[slot, 0])]
-        if both:
-            copies.append(pltpu.make_async_copy(wg.at[layer, :, columns], wgu.at[slot, :, pl.ds(0, FC)], w_sem.at[slot, 1]))
-            copies.append(pltpu.make_async_copy(wu.at[layer, :, columns], wgu.at[slot, :, pl.ds(FC, FC)], w_sem.at[slot, 2]))
-        return copies
+        return [
+            pltpu.make_async_copy(w.at[layer, :, columns], wgu.at[slot, :, pl.ds(i * FC, FC)], w_sem.at[slot, i]) for i, w in enumerate((wg, wu))
+        ]
 
     def rows_of(t):
         return pl.ds(pl.multiple_of(t * TB, TB), TB)
@@ -378,6 +383,12 @@
     def derivatives(c, t):
         return pltpu.make_async_copy(by0.at[c - NF, rows_of(t), :], by_a.at[rows_of(t), :], by_sem.at[t])
 
+    def keep_dgu(c, t):
+        return pltpu.make_async_copy(dgu.at[rows_of(t), :], kept_dgu.at[c, rows_of(t), :], dgu_sem.at[t])
+
+    def fetch_dgu(c, t):
+        return pltpu.make_async_copy(kept_dgu.at[c, rows_of(t), :], dgu.at[rows_of(t), :], dgu_sem.at[t])
+
     def hidden(c):
         return pltpu.make_async_copy(hid0.at[c - NF], hid, load_sem.at[2])
 
@@ -385,7 +396,7 @@
     load_a0 = pltpu.make_async_copy(a0, a, load_sem.at[1])
 
     total.arrive()
-    for copy in weights(0, True) + first_rows(0):
+    for copy in down_weights(0) + input_weights(0) + first_rows(0):
         copy.start()
     by_a[:, :D] = jnp.zeros((T, D), F32)
     total.meet()
@@ -453,17 +464,17 @@
 
     def last_layer(c, carry):
         slot = lax.rem(c, 2)
-        for copy in weights(c, True):
+        for copy in down_weights(c) + input_weights(c):
             copy.wait()
 
         @pl.when(jnp.logical_and(c > 0, c < NF - 1))
         def _():
-            for copy in weights(c + 1, True):
+            for copy in down_weights(c + 1) + input_weights(c + 1):
                 copy.start()
 
         @pl.when(c == NF - 1)
         def _():
-            for copy in weights(c + 1, False):
+            for copy in down_weights(c + 1):
                 copy.start()
 
         def block(t, carry):
@@ -479,8 +490,12 @@
 
                 @pl.when(t == NT - 1)
                 def _():
-                    for copy in weights(1, True):
+                    for copy in down_weights(1) + input_weights(1):
                         copy.start()
+
+            @pl.when(c > 0)
+            def _():
+                keep_dgu(c - 1, t).wait()
 
             rows = rows_of(t)
             gu = dot(a[rows, :], wgu[slot], 1, 0)
@@ -488,6 +503,11 @@
             hid[rows, :], by_gate, by_up = gated(gu[:, :FC], gu[:, FC:])
             dgu[rows, :FC] = (by_hidden * by_gate).astype(BF)
             dgu[rows, FC:] = (by_hidden * by_up).astype(BF)
+
+            @pl.when(c < NF - 1)
+            def _():
+                keep_dgu(c, t).start()
+
             sends_of_block(t, c, LAST)
             return carry
 
@@ -495,27 +515,57 @@
 
         weight_gradients(c, LAST)
 
-        @pl.when(c == NF - 1)
-        def _():
-            load_h1.start()
+        return carry
+
+    lax.fori_loop(0, NF, last_layer, 0)
+    load_h1.start()
+
+    def sends_between(step):
+        for n in range(10):
+            if (BETWEEN, n) in PLAN:
+
+                @pl.when(step == n)
+                def _(n=n):
+                    for k, q, parts, chunk in sorted(PLAN[BETWEEN, n], key=first):
+                        total.step(k, q, parts, chunk, chunk >= NG)
+
+    def input_chunk(n, carry):
+        c = NF - 1 - n
+        slot = lax.rem(c, 2)
+
+        @pl.when(n >= 2)
+        def _():
+            for copy in input_weights(c):
+                copy.wait()
+
+        @pl.when(jnp.logical_and(n >= 1, c > 0))
+        def _():
+            for copy in input_weights(c - 1):
+                copy.start()
 
         def input_block(t, carry):
+            @pl.when(n >= 1)
+            def _():
+                fetch_dgu(c, t).wait()
+
             input_rows(t, slot)
 
-            @pl.when(t == 1)
-            def _():
-                sends(7, c, LAST)
-
-            @pl.when(t == 3)
-            def _():
-                sends(8, c, LAST)
+            @pl.when(c > 0)
+            def _():
+                fetch_dgu(c - 1, t).start()
+
+            pair, odd = split(t, 2)
+
+            @pl.when(odd == 1)
+            def _():
+                sends_between(2 * n + pair)
 
             return carry
 
-        lax.fori_loop(0, jnp.where(c < NF - 1, NT, 1), input_block, 0)
+        lax.fori_loop(0, jnp.where(c > 0, NT, 1), input_block, 0)
         return carry
 
-    lax.fori_loop(0, NF, last_layer, 0)
+    lax.fori_loop(0, NF, input_chunk, 0)
     load_h1.wait()
 
     def norm_rows(t):
@@ -528,17 +578,16 @@
             by_h[rows, :] = (by_h[rows, :].astype(F32) + through.astype(BF).astype(F32)).astype(BF)
 
     def norm_block(t, carry):
+        fetch_dgu(0, t).wait()
         norm_rows(t - 1)
-        input_rows(t, (NF - 1) % 2)
+        input_rows(t, 0)
         derivatives(NF, t - 1).start()
 
-        @pl.when(t == 1)
-        def _():
-            sends(7, NF - 1, LAST[-1:])
-
-        @pl.when(t == 3)
-        def _():
-            sends(8, NF - 1, LAST[-1:])
+        pair, odd = split(t, 2)
+
+        @pl.when(odd == 1)
+        def _():
+            sends_between(2 * (NF - 1) + pair)
 
         return carry
 
@@ -549,12 +598,12 @@
 
     def first_layer(c, carry):
         slot = lax.rem(c, 2)
-        for copy in weights(c, False):
+        for copy in down_weights(c):
             copy.wait()
 
         @pl.when(c < NC - 1)
         def _():
-            for copy in weights(c + 1, False):
+            for copy in down_weights(c + 1):
                 copy.start()
 
         def block(t, carry):
@@ -592,9 +641,9 @@
     dma = pltpu.SemaphoreType.DMA
     return pl.pallas_call(
         backward_kernel,
-        out_shape=[jax.ShapeDtypeStruct(shape, BF) for shape in ((2, D, FF), (2, D, FF), (2, FF, D), (NK, 3, D // 16, FC))],
+        out_shape=[jax.ShapeDtypeStruct(shape, BF) for shape in ((2, D, FF), (2, D, FF), (2, FF, D), (NK, 3, D // 16, FC), (NF - 1, T, 2 * FC))],
         in_specs=any_spec(9),
-        out_specs=any_spec(4),
+        out_specs=any_spec(5),
         scratch_shapes=[
             pltpu.VMEM((T, D), BF),
             pltpu.VMEM((T, D), BF),
@@ -614,6 +663,7 @@
             dma((3,)),
             dma((2, 3)),
             dma((NT,)),
+            dma((NT,)),
             dma((RS, 3, 4)),
             dma((RS, 3, 4)),
             dma((NG, 3, 7)),
@@ -622,13 +672,13 @@
             pltpu.SemaphoreType.REGULAR((4, 2)),
         ],
         compiler_params=pltpu.CompilerParams(collective_id=0, has_side_effects=True, vmem_limit_bytes=VMEM_LIMIT),
-        cost_estimate=pl.CostEstimate(flops=24 * T * D * FF, bytes_accessed=200 * 2**20, transcendentals=2 * T * FF),
+        cost_estimate=pl.CostEstimate(flops=24 * T * D * FF, bytes_accessed=200 << 20, transcendentals=2 * T * FF),
         name="backward",
     )(a1, a0, dy, h1, by0, hid0, wg, wu, wd)
 
 
 SLOTS = 4
-QUARTERS = ((D // 4, FC), (D // 4, FC), (FC // 4, D))
+HALVES = ((D // 2, FC), (D // 2, FC), (FC // 2, D))
 
 
 def adamw(w, m, v, g):
@@ -648,53 +698,47 @@
     n_g = 1 if in_pieces else 3
     g, outs = refs[9 : 9 + n_g], refs[9 + n_g + n_before : 18 + n_g + n_before]
     *bufs, load_sem, store_sem = refs[18 + n_g + n_before :]
-    units = 4 * len(chunks)
-
-    def window(ref, p, c, q):
-        rows, columns = QUARTERS[p]
+    units, units_before = 2 * len(chunks), 2 * chunks[0]
+
+    def window(ref, p, c, half):
+        rows, columns = HALVES[p]
         layer, start = layer_and_start(c)
         if p < 2:
-            return ref.at[layer, pl.ds(pl.multiple_of(q * rows, rows), rows), pl.ds(pl.multiple_of(start, 128), FC)]
-        return ref.at[layer, pl.ds(pl.multiple_of(start + q * rows, 32), rows), :]
-
-    def gradient(p, c, q, to, sem):
+            return ref.at[layer, pl.ds(pl.multiple_of(half * rows, rows), rows), pl.ds(pl.multiple_of(start, 128), FC)]
+        return ref.at[layer, pl.ds(pl.multiple_of(start + half * rows, 64), rows), :]
+
+    def gradient(p, c, half, to, sem):
         if not in_pieces:
-            return [pltpu.make_async_copy(window(g[p], p, c, q), to, sem)]
-        half, low = split(q, 2)
-        if p < 2:
-            return [
-                pltpu.make_async_copy(g[0].at[owner(p, half, e) + low * ORDER[p][1], c - NG, p], to.at[pl.ds(64 * e, 64), :], sem) for e in range(4)
-            ]
+            return [pltpu.make_async_copy(window(g[p], p, c, half), to, sem)]
         copies = []
         for e in range(8):
-            piece, columns = g[0].at[owner(p, half, e), c - NG, p], pl.ds(128 * e, 128)
-            for b, rows, src, dst in ((3 * low, 64, 0, 32 * low), (1 + 3 * low, 64, 0, 64 + 32 * low), (2, 32, 32 * low, 128 - 128 * low)):
-                there = pl.ds(pl.multiple_of(128 * b, 128), 128)
-                copies.append(
-                    pltpu.make_async_copy(
-                        piece.at[pl.ds(at(src, 32), rows), there], to.at[pl.ds(pl.multiple_of(dst, 32), rows), columns], sem
-                    )
-                )
+            piece = g[0].at[owner(p, half, e), c - NG, p]
+            if p < 2:
+                copies.append(pltpu.make_async_copy(piece, to.at[pl.ds(64 * e, 64), :], sem))
+            else:
+                for b in range(5):
+                    there = to.at[pl.ds(64 * b, 64), pl.ds(128 * e, 128)]
+                    copies.append(pltpu.make_async_copy(piece.at[:, pl.ds(128 * b, 128)], there, sem))
         return copies
 
     def loads(n, act):
-        (c, q), slot = split(n + 4 * chunks[0], 4), lax.rem(n, SLOTS)
+        (c, half), slot = split(n + units_before, 2), lax.rem(n, SLOTS)
         for p in range(3):
             for b, ref in enumerate((w[p], m[p], v[p])):
-                copy = pltpu.make_async_copy(window(ref, p, c, q), bufs[4 * p + b].at[slot], load_sem.at[slot, p, b])
+                copy = pltpu.make_async_copy(window(ref, p, c, half), bufs[4 * p + b].at[slot], load_sem.at[slot, p, b])
                 copy.start() if act == "start" else copy.wait()
             to, sem = bufs[4 * p + 3].at[slot], load_sem.at[slot, p, 3]
             if act == "start":
-                for copy in gradient(p, c, q, to, sem):
+                for copy in gradient(p, c, half, to, sem):
                     copy.start()
             else:
-                pltpu.make_async_copy(window(w[p], p, c, q), to, sem).wait()
+                pltpu.make_async_copy(window(w[p], p, c, half), to, sem).wait()
 
     def stores(n, act):
-        (c, q), slot = split(n + 4 * chunks[0], 4), lax.rem(n, SLOTS)
+        (c, half), slot = split(n + units_before, 2), lax.rem(n, SLOTS)
         for p in range(3):
             for b in range(3):
-                copy = pltpu.make_async_copy(bufs[4 * p + b].at[slot], window(outs[3 * b + p], p, c, q), store_sem.at[slot, p, b])
+                copy = pltpu.make_async_copy(bufs[4 * p + b].at[slot], window(outs[3 * b + p], p, c, half), store_sem.at[slot, p, b])
                 copy.start() if act == "start" else copy.wait()
 
     loads(0, "start")
@@ -707,11 +751,12 @@
         def _():
             stores(n - 2, "wait")
 
+        loads(n, "wait")
+
         @pl.when(n + 2 < units)
         def _():
             loads(n + 2, "start")
 
-        loads(n, "wait")
         for p in range(3):
             block = 64 if p < 2 else 32
 
@@ -722,7 +767,7 @@
                 )
                 return carry
 
-            lax.fori_loop(0, QUARTERS[p][0] // block, rows_block, 0)
+            lax.fori_loop(0, HALVES[p][0] // block, rows_block, 0)
         stores(n, "start")
         return carry
 
@@ -744,7 +789,7 @@
         in_specs=any_spec(n_in + n_before),
         out_specs=any_spec(9),
         input_output_aliases={n_in + i: i for i in range(n_before)},
-        scratch_shapes=[pltpu.VMEM((SLOTS, *shape), t) for shape in QUARTERS for t in (BF, F32, F32, BF)]
+        scratch_shapes=[pltpu.VMEM((SLOTS, *shape), t) for shape in HALVES for t in (BF, F32, F32, BF)]
         + [pltpu.SemaphoreType.DMA((SLOTS, 3, 4)), pltpu.SemaphoreType.DMA((SLOTS, 3, 3))],
         compiler_params=pltpu.CompilerParams(vmem_limit_bytes=VMEM_LIMIT),
         cost_estimate=pl.CostEstimate(flops=15 * elements, bytes_accessed=22 * elements, transcendentals=elements),
@@ -756,7 +801,7 @@
     def step(x, dy, *arrays):
         weights = arrays[:3]
         by0, hid0, h1, a1, a0 = forward(x[0], *weights)
-        *gradients, pieces = backward(a1, a0, dy[0], h1, by0, hid0, *weights)
+        *gradients, pieces, _ = backward(a1, a0, dy[0], h1, by0, hid0, *weights)
         gathered = lax.all_gather(pieces, "dp")
         new = adamw_call(range(NG), arrays, gradients)
         return tuple(adamw_call(range(NG, NC), arrays, (gathered,), new))

time: 467 us -> 462 us (0.989)
  no operation moved by 1% of the time
where the time goes in v3:
time: 462 us
  Pallas kernels  448 us (97%)
  between operations  14.1 us (3%)
    pallas_call x1, Pallas kernels, backward(): pl.pallas_call(backward_kernel, out_shape=[jax.ShapeDtypeStruct(shape, BF...  255 us
    pallas_call x2, Pallas kernels, adamw_call(): pl.pallas_call(kernel, out_shape=[jax.ShapeDtypeStruct(a.shape, a.dtype)...  137 us
    pallas_call x1, Pallas kernels, forward(): pl.pallas_call(forward_kernel, grid=(NT,), out_shape=[jax.ShapeDtypeStruc...  56.3 us
  transfers between devices with their start and end apart: 1, of which 0 were waited for; matrix products, arithmetic and copies ran while one was open for 0% of the time, Pallas kernels for 18%

profile of v3, /device:TPU:0, one launch (start us, length us, event | category | flops | bytes accessed | tf_op | source)
XLA Modules:
  0.0 462.1 jit_solution(15774086341876032593)
XLA Ops:
  7.2 0.0 all-gather.3.cloned.1.call-start
  7.2 56.3 %forward.1 = (f32[5,2048,1280]{2,1,0:T(8,128)}, bf16[5,2048,640]{2,1,0:T(8,128)(2,1)}, bf16[2048,1024]{1,0:T(8,128)(2,1)}, bf16[2048,1024]{1,0:T(8,128)(2,1)}, bf16[2048,1024]{1,0:T(8,128)(2,1)}) custom-call(bf16[2048,1024]{1,0:T(8,128)(2,1)} %bitcast.4, bf16[2,1024,3200]{2,1,0:T(8,128)(2,1)} %refs_0_.3, bf16[2,1024,3200]{2,1,0:T(8,128)(2,1)} %refs_1_.3, ...), custom_call_target="tpu_custom_call" | custom-call | flops 40265318400 | bytes 115343360 | tf_op jit(solution)/shard_map/forward/pallas_call | solution.py:117
  63.6 254.7 %backward.1 = (bf16[2,1024,3200]{2,1,0:T(8,128)(2,1)}, bf16[2,1024,3200]{2,1,0:T(8,128)(2,1)}, bf16[2,3200,1024]{2,1,0:T(8,128)(2,1)}, bf16[4,3,64,640]{3,2,1,0:T(8,128)(2,1)}, bf16[4,2048,1280]{2,1,0:T(8,128)(2,1)}) custom-call(bf16[2048,1024]{1,0:T(8,128)(2,1)} %get-tuple-element.27.a1, bf16[2048,1024]{1,0:T(8,128)(2,1)} %get-tuple-element.28.a0, ...), custom_call_target="tpu_custom_call" | custom-call | flops 161061273600 | bytes 209715200 | tf_op jit(solution)/shard_map/backward/pallas_call | solution.py:642
  318.3 0.0 all-gather.3.cloned.1.call-update
  318.3 81.9 %adamw_whole.1 = (bf16[2,1024,3200]{2,1,0:T(8,128)(2,1)}, bf16[2,1024,3200]{2,1,0:T(8,128)(2,1)}, bf16[2,3200,1024]{2,1,0:T(8,128)(2,1)}, f32[2,1024,3200]{2,1,0...) custom-call(bf16[2,1024,3200]{2,1,0:T(8,128)(2,1)} %refs_0_.3, ...), custom_call_target="tpu_custom_call" | custom-call | flops 176947200 | bytes 259522560 | tf_op jit(solution)/shard_map/adamw_whole/pallas_call | solution.py:786
  400.2 0.0 all-gather.3.cloned.1.call-done
  400.3 55.0 %adamw_pieces.1 = (bf16[2,1024,3200]{2,1,0:T(8,128)(2,1)}, bf16[2,1024,3200]{2,1,0:T(8,128)(2,1)}, bf16[2,3200,1024]{2,1,0:T(8,128)(2,1)}, f32[2,1024,3200]{2,1,...) custom-call(bf16[2,1024,3200]{2,1,0:T(8,128)(2,1)} %refs_0_.3, ...), custom_call_target="tpu_custom_call", output_to_operand_aliasing={{0}: (10, {}), {1}: (11, {}), {2}: (12, {}), {3}: (13, {}),... | custom-call | flops 117964800 | bytes 173015040 | tf_op jit(solution)/shard_map/adamw_pieces/pallas_call | solution.py:786
Async XLA Ops:
  7.2 393.1 %all-gather.3.cloned.1.call-start = ((), (), s32[]{:S(2)}) async-start(), calls=%async_computation | async-start | bytes 16711680 | tf_op jit(solution)/shard_map/all_gather | solution.py:805
Sparse Core Ops, SparseCore 0:
  318.4 71.9 all-gather.2

commit v4 on v3

--- a/solution.py
+++ b/solution.py
@@ -15,8 +15,8 @@
 NG = NF + 1
 NK = NC - NG
 BETWEEN = -1
-RS = 2
-VMEM_LIMIT = 63 << 20
+RS = 3
+VMEM_LIMIT = 67043328
 
 AXES = (1, 8, 4, 2)
 ORDER = (AXES, (1, 4, 2, 8), (1, 2, 8, 4))
@@ -49,7 +49,7 @@
     return [pl.BlockSpec(memory_space=pl.ANY)] * n
 
 
-def forward_kernel(x_ref, wg, wu, wd, by0, hid0, h1_ref, a1_ref, a0_ref, wgu, wdv, hid, byb, wsem, dsem, osem, hsem):
+def forward_kernel(x, wg, wu, wd, by0, hid0, h1_ref, a1_ref, a0_ref, xb, wgu, wdv, hid, byb, xsem, wsem, dsem, osem, hsem):
     i = pl.program_id(0)
     rows = pl.ds(pl.multiple_of(i * TB, TB), TB)
 
@@ -64,8 +64,12 @@
 
     down = pltpu.make_async_copy(wd.at[0], wdv, dsem)
 
+    def tokens(n):
+        return pltpu.make_async_copy(x.at[pl.ds(pl.multiple_of(n * TB, TB), TB), :], xb.at[lax.rem(n, 2)], xsem.at[lax.rem(n, 2)])
+
     @pl.when(i == 0)
     def _():
+        tokens(i).start()
         for c in range(NF):
             for copy in weights(c):
                 copy.start()
@@ -77,7 +81,13 @@
     def out_hid(c):
         return pltpu.make_async_copy(hid.at[:, columns(c)], hid0.at[c, rows, :], hsem.at[c])
 
-    wide = x_ref[...].astype(F32)
+    tokens(i).wait()
+
+    @pl.when(i < NT - 1)
+    def _():
+        tokens(i + 1).start()
+
+    wide = xb[lax.rem(i, 2)].astype(F32)
     a0_ref[...] = (wide * inverse_rms(wide)).astype(BF)
 
     def chunk(c, carry):
@@ -102,7 +112,7 @@
     def _():
         down.wait()
 
-    h1_ref[...] = (x_ref[...].astype(F32) + dot(hid[...], wdv[...], 1, 0).astype(BF).astype(F32)).astype(BF)
+    h1_ref[...] = (xb[lax.rem(i, 2)].astype(F32) + dot(hid[...], wdv[...], 1, 0).astype(BF).astype(F32)).astype(BF)
     wide1 = h1_ref[...].astype(F32)
     a1_ref[...] = (wide1 * inverse_rms(wide1)).astype(BF)
     for c in range(NF):
@@ -124,13 +134,15 @@
             jax.ShapeDtypeStruct((T, D), BF),
             jax.ShapeDtypeStruct((T, D), BF),
         ],
-        in_specs=[rows] + any_spec(3),
+        in_specs=any_spec(4),
         out_specs=any_spec(2) + [rows] * 3,
         scratch_shapes=[
+            pltpu.VMEM((2, TB, D), BF),
             pltpu.VMEM((NF, D, 2 * FC), BF),
             pltpu.VMEM((FF, D), BF),
             pltpu.VMEM((TB, FF), BF),
             pltpu.VMEM((2, TB, 2 * FC), F32),
+            dma((2,)),
             dma((NF, 2)),
             dma,
             dma((2,)),
@@ -318,16 +330,16 @@
 DIGITS = "0123456789abcdefghijklmnopqrstuvwxyzABCDEFGHIJKLMNOPQRSTUVWXYZ"
 STAGES = [(k, q) for k in range(9) for q in range(4 if k == 6 else 1)]
 TIMES = (
-    ("57bdgirDFJUX", "46acehkvvJRX"),
-    ("56adginrvBIM", "45acehrtvwJP"),
-    ("56adginrvAIM", "45acehrtvvJP"),
-    ("57bdgmootzBQ", "45adglnotOSX"),
-    ("57adekrtyJRW", "46aefgmstyOX"),
-    ("56bcfinrttCE", "46bcdhmsvxBH"),
-    ("56behi", "45adgh"),
-    ("58cegi", "48cegh"),
-    ("58gouA", "57gsxF"),
-    ("58bmCV", "47bmFW"),
+    ("57bdgjoxGOTV", "45begjlCHKPV"),
+    ("57bdgjnnrxJQ", "47bdfjmrsDMU"),
+    ("57bdgjnnrwJQ", "47bdfjmrsDMU"),
+    ("56bdhkmmotxL", "57bdfimnszOW"),
+    ("56bdfhqsswBQ", "46behjnopxIN"),
+    ("56bdfjpqqryD", "45adijopqsxR"),
+    ("57beko", "46beho"),
+    ("58iqAD", "48fpBF"),
+    ("56cpCE", "45bqzD"),
+    ("59dkEO", "48clBW"),
 )
 
 
@@ -569,13 +581,16 @@
     load_h1.wait()
 
     def norm_rows(t):
-        for half in range(2):
-            rows = pl.ds(pl.multiple_of(t * TB + half * (TB // 2), TB // 2), TB // 2)
+        def some(n, carry):
+            rows = pl.ds(pl.multiple_of(t * TB + n * 128, 128), 128)
             wide = a[rows, :].astype(F32)
             scale = inverse_rms(wide)
             by_normed = by_a[rows, :D].astype(BF).astype(F32)
             through = by_normed * scale - wide * (scale * scale * scale * jnp.mean(by_normed * wide, -1, keepdims=True))
             by_h[rows, :] = (by_h[rows, :].astype(F32) + through.astype(BF).astype(F32)).astype(BF)
+            return carry
+
+        lax.fori_loop(0, TB // 128, some, 0)
 
     def norm_block(t, carry):
         fetch_dgu(0, t).wait()

time: 462 us -> 457 us (0.989)
  Pallas kernels: 448 us -> 443 us
    pallas_call x1, Pallas kernels: 255 us -> 250 us  [backward(): pl.pallas_call(backward_kernel, out_shape=[jax.ShapeDtypeStruct(shape, BF...]
where the time goes in v4:
time: 457 us
  Pallas kernels  443 us (97%)
  between operations  14.1 us (3%)
    pallas_call x1, Pallas kernels, backward(): pl.pallas_call(backward_kernel, out_shape=[jax.ShapeDtypeStruct(shape, BF...  250 us
    pallas_call x2, Pallas kernels, adamw_call(): pl.pallas_call(kernel, out_shape=[jax.ShapeDtypeStruct(a.shape, a.dtype)...  137 us
    pallas_call x1, Pallas kernels, forward(): pl.pallas_call(forward_kernel, grid=(NT,), out_shape=[jax.ShapeDtypeStruc...  55.9 us
  transfers between devices with their start and end apart: 1, of which 0 were waited for; matrix products, arithmetic and copies ran while one was open for 0% of the time, Pallas kernels for 18%

profile of v4, /device:TPU:0, one launch (start us, length us, event | category | flops | bytes accessed | tf_op | source)
XLA Modules:
  0.0 456.9 jit_solution(5644563342937578170)
XLA Ops:
  7.2 0.0 all-gather.3.cloned.1.call-start
  7.2 55.9 %forward.1 = (f32[5,2048,1280]{2,1,0:T(8,128)}, bf16[5,2048,640]{2,1,0:T(8,128)(2,1)}, bf16[2048,1024]{1,0:T(8,128)(2,1)}, bf16[2048,1024]{1,0:T(8,128)(2,1)}, bf16[2048,1024]{1,0:T(8,128)(2,1)}) custom-call(bf16[2048,1024]{1,0:T(8,128)(2,1)} %bitcast.4, bf16[2,1024,3200]{2,1,0:T(8,128)(2,1)} %refs_0_.3, bf16[2,1024,3200]{2,1,0:T(8,128)(2,1)} %refs_1_.3, ...), custom_call_target="tpu_custom_call" | custom-call | flops 40265318400 | bytes 115343360 | tf_op jit(solution)/shard_map/forward/pallas_call | solution.py:127
  63.1 250.0 %backward.1 = (bf16[2,1024,3200]{2,1,0:T(8,128)(2,1)}, bf16[2,1024,3200]{2,1,0:T(8,128)(2,1)}, bf16[2,3200,1024]{2,1,0:T(8,128)(2,1)}, bf16[4,3,64,640]{3,2,1,0:T(8,128)(2,1)}, bf16[4,2048,1280]{2,1,0:T(8,128)(2,1)}) custom-call(bf16[2048,1024]{1,0:T(8,128)(2,1)} %get-tuple-element.27.a1, bf16[2048,1024]{1,0:T(8,128)(2,1)} %get-tuple-element.28.a0, ...), custom_call_target="tpu_custom_call" | custom-call | flops 161061273600 | bytes 209715200 | tf_op jit(solution)/shard_map/backward/pallas_call | solution.py:657
  313.1 0.0 all-gather.3.cloned.1.call-update
  313.1 81.9 %adamw_whole.1 = (bf16[2,1024,3200]{2,1,0:T(8,128)(2,1)}, bf16[2,1024,3200]{2,1,0:T(8,128)(2,1)}, bf16[2,3200,1024]{2,1,0:T(8,128)(2,1)}, f32[2,1024,3200]{2,1,0...) custom-call(bf16[2,1024,3200]{2,1,0:T(8,128)(2,1)} %refs_0_.3, ...), custom_call_target="tpu_custom_call" | custom-call | flops 176947200 | bytes 259522560 | tf_op jit(solution)/shard_map/adamw_whole/pallas_call | solution.py:801
  395.0 0.0 all-gather.3.cloned.1.call-done
  395.1 55.0 %adamw_pieces.1 = (bf16[2,1024,3200]{2,1,0:T(8,128)(2,1)}, bf16[2,1024,3200]{2,1,0:T(8,128)(2,1)}, bf16[2,3200,1024]{2,1,0:T(8,128)(2,1)}, f32[2,1024,3200]{2,1,...) custom-call(bf16[2,1024,3200]{2,1,0:T(8,128)(2,1)} %refs_0_.3, ...), custom_call_target="tpu_custom_call", output_to_operand_aliasing={{0}: (10, {}), {1}: (11, {}), {2}: (12, {}), {3}: (13, {}),... | custom-call | flops 117964800 | bytes 173015040 | tf_op jit(solution)/shard_map/adamw_pieces/pallas_call | solution.py:801
Async XLA Ops:
  7.2 387.9 %all-gather.3.cloned.1.call-start = ((), (), s32[]{:S(2)}) async-start(), calls=%async_computation | async-start | bytes 16711680 | tf_op jit(solution)/shard_map/all_gather | solution.py:820
Sparse Core Ops, SparseCore 0:
  313.2 71.9 all-gather.2

commit v5 on v4

--- a/solution.py
+++ b/solution.py
@@ -330,16 +330,16 @@
 DIGITS = "0123456789abcdefghijklmnopqrstuvwxyzABCDEFGHIJKLMNOPQRSTUVWXYZ"
 STAGES = [(k, q) for k in range(9) for q in range(4 if k == 6 else 1)]
 TIMES = (
-    ("57bdgjoxGOTV", "45begjlCHKPV"),
-    ("57bdgjnnrxJQ", "47bdfjmrsDMU"),
-    ("57bdgjnnrwJQ", "47bdfjmrsDMU"),
-    ("56bdhkmmotxL", "57bdfimnszOW"),
-    ("56bdfhqsswBQ", "46behjnopxIN"),
-    ("56bdfjpqqryD", "45adijopqsxR"),
-    ("57beko", "46beho"),
-    ("58iqAD", "48fpBF"),
-    ("56cpCE", "45bqzD"),
-    ("59dkEO", "48clBW"),
+    ("57bdfjovBMRX", "47cehjorIJRV"),
+    ("57bdgjpqtwJV", "57bdhjpqstJS"),
+    ("57bdgjpqtvJV", "57bdhjpqstJS"),
+    ("57bfilnootOV", "47beglorszBN"),
+    ("57bdfgmqrxRT", "45adgjoopxCF"),
+    ("57cgijnnnsxO", "45adgjppqqAW"),
+    ("56belo", "45bdkl"),
+    ("57imzB", "57ipxH"),
+    ("56cmrA", "57cltz"),
+    ("57dgPR", "46chHP"),
 )
 
 
@@ -582,7 +582,7 @@
 
     def norm_rows(t):
         def some(n, carry):
-            rows = pl.ds(pl.multiple_of(t * TB + n * 128, 128), 128)
+            rows = pl.ds(pl.multiple_of(t * TB + n * 256, 256), 256)
             wide = a[rows, :].astype(F32)
             scale = inverse_rms(wide)
             by_normed = by_a[rows, :D].astype(BF).astype(F32)
@@ -590,7 +590,7 @@
             by_h[rows, :] = (by_h[rows, :].astype(F32) + through.astype(BF).astype(F32)).astype(BF)
             return carry
 
-        lax.fori_loop(0, TB // 128, some, 0)
+        lax.fori_loop(0, TB // 256, some, 0)
 
     def norm_block(t, carry):
         fetch_dgu(0, t).wait()

time: 457 us -> 456 us (level)
  no operation moved by 1% of the time
where the time goes in v5:
time: 456 us
  Pallas kernels  441 us (97%)
  between operations  14.1 us (3%)
    pallas_call x1, Pallas kernels, backward(): pl.pallas_call(backward_kernel, out_shape=[jax.ShapeDtypeStruct(shape, BF...  249 us
    pallas_call x2, Pallas kernels, adamw_call(): pl.pallas_call(kernel, out_shape=[jax.ShapeDtypeStruct(a.shape, a.dtype)...  137 us
    pallas_call x1, Pallas kernels, forward(): pl.pallas_call(forward_kernel, grid=(NT,), out_shape=[jax.ShapeDtypeStruc...  55.9 us
  transfers between devices with their start and end apart: 1, of which 0 were waited for; matrix products, arithmetic and copies ran while one was open for 0% of the time, Pallas kernels for 18%

profile of v5, /device:TPU:0, one launch (start us, length us, event | category | flops | bytes accessed | tf_op | source)
XLA Modules:
  0.0 455.6 jit_solution(602558006257735102)
XLA Ops:
  7.2 0.0 all-gather.3.cloned.1.call-start
  7.2 55.9 %forward.1 = (f32[5,2048,1280]{2,1,0:T(8,128)}, bf16[5,2048,640]{2,1,0:T(8,128)(2,1)}, bf16[2048,1024]{1,0:T(8,128)(2,1)}, bf16[2048,1024]{1,0:T(8,128)(2,1)}, bf16[2048,1024]{1,0:T(8,128)(2,1)}) custom-call(bf16[2048,1024]{1,0:T(8,128)(2,1)} %bitcast.4, bf16[2,1024,3200]{2,1,0:T(8,128)(2,1)} %refs_0_.3, bf16[2,1024,3200]{2,1,0:T(8,128)(2,1)} %refs_1_.3, ...), custom_call_target="tpu_custom_call" | custom-call | flops 40265318400 | bytes 115343360 | tf_op jit(solution)/shard_map/forward/pallas_call | solution.py:127
  63.1 248.6 %backward.1 = (bf16[2,1024,3200]{2,1,0:T(8,128)(2,1)}, bf16[2,1024,3200]{2,1,0:T(8,128)(2,1)}, bf16[2,3200,1024]{2,1,0:T(8,128)(2,1)}, bf16[4,3,64,640]{3,2,1,0:T(8,128)(2,1)}, bf16[4,2048,1280]{2,1,0:T(8,128)(2,1)}) custom-call(bf16[2048,1024]{1,0:T(8,128)(2,1)} %get-tuple-element.27.a1, bf16[2048,1024]{1,0:T(8,128)(2,1)} %get-tuple-element.28.a0, ...), custom_call_target="tpu_custom_call" | custom-call | flops 161061273600 | bytes 209715200 | tf_op jit(solution)/shard_map/backward/pallas_call | solution.py:657
  311.7 0.0 all-gather.3.cloned.1.call-update
  311.7 81.9 %adamw_whole.1 = (bf16[2,1024,3200]{2,1,0:T(8,128)(2,1)}, bf16[2,1024,3200]{2,1,0:T(8,128)(2,1)}, bf16[2,3200,1024]{2,1,0:T(8,128)(2,1)}, f32[2,1024,3200]{2,1,0...) custom-call(bf16[2,1024,3200]{2,1,0:T(8,128)(2,1)} %refs_0_.3, ...), custom_call_target="tpu_custom_call" | custom-call | flops 176947200 | bytes 259522560 | tf_op jit(solution)/shard_map/adamw_whole/pallas_call | solution.py:801
  393.7 0.0 all-gather.3.cloned.1.call-done
  393.7 55.0 %adamw_pieces.1 = (bf16[2,1024,3200]{2,1,0:T(8,128)(2,1)}, bf16[2,1024,3200]{2,1,0:T(8,128)(2,1)}, bf16[2,3200,1024]{2,1,0:T(8,128)(2,1)}, f32[2,1024,3200]{2,1,...) custom-call(bf16[2,1024,3200]{2,1,0:T(8,128)(2,1)} %refs_0_.3, ...), custom_call_target="tpu_custom_call", output_to_operand_aliasing={{0}: (10, {}), {1}: (11, {}), {2}: (12, {}), {3}: (13, {}),... | custom-call | flops 117964800 | bytes 173015040 | tf_op jit(solution)/shard_map/adamw_pieces/pallas_call | solution.py:801
Async XLA Ops:
  7.2 386.5 %all-gather.3.cloned.1.call-start = ((), (), s32[]{:S(2)}) async-start(), calls=%async_computation | async-start | bytes 16711680 | tf_op jit(solution)/shard_map/all_gather | solution.py:820
Sparse Core Ops, SparseCore 0:
  311.9 72.0 all-gather.2
